TPU v7x, 128 devices: a whole 4x4x4 slice. The times are simulated.
128 devices in a mesh: dp: 8 (over z, core), mp: 16 (over y, x).
Axes of the slice: x: 4, y: 4, z: 4, core: 2. Of those that a mesh axis runs over, the one named last changes fastest.
Arguments:
- crop_hidden: bfloat16 [8, 1536, 8192], P(None, 'dp', 'mp'), may hold values from -15 to 15
- projector_weight: bfloat16 [8192, 8192], P('mp'), may hold values from -0.21213203 to 0.21213203
- pairing: int32 [8, 1536], P(None, 'dp'), may hold values from 0 to 191, as said below
Outputs:
- embeddings: float32 [8192, 8, 1536], P('mp', 'dp')
- loss_terms: float32 [4], replicated
Inputs may be any that keep to these rules, and one draw needn't show every extreme that they name: Each aligned block of 192 entries of a row of pairing is a permutation of 0 to 191.
All inputs are finite; a program needn't handle non-finite values.
Results may differ from a plain program's by a relative error of at most 0.0003.
Values may be sent and summed in bfloat16 or wider, within the bound.
No kernel may reach another device: no remote copies, remote signals or barrier semaphores. Data moves between devices by JAX's collectives and lax.ppermute only.
A program may use at most 128 MiB of HBM per device.

v0:
```python
import jax
import jax.numpy as jnp
from jax import lax
from jax.experimental import pallas as pl
from jax.experimental.pallas import tpu as pltpu
from jax.sharding import Mesh
from jax.sharding import PartitionSpec as P

MP = ("mp_0", "mp_1")
DP = ("dp_0", "dp_1")
AXES = ("mp_0", "mp_1", "dp_0", "dp_1")
RING = 4


epsilon = 0.0001
GRAM_BLOCK = 128


def shift(x, axis, step):
    return lax.ppermute(x, axis, [(i, (i + step) % RING) for i in range(RING)])


def swap(x):
    return lax.ppermute(x, "dp_1", [(0, 1), (1, 0)])


def assemble_body(places, *refs):
    parts, out = refs[:-1], refs[-1]
    rows = parts[0].shape[1]

    def step(i, carry):
        for n, part in enumerate(parts):
            start = pl.multiple_of(places[n] * rows, rows)
            out[i, pl.ds(start, rows), :] = part[i]
        return carry

    lax.fori_loop(0, out.shape[0], step, 0)


def assemble(parts, places):
    count, rows, width = parts[0].shape
    vmem = pl.BlockSpec(memory_space=pltpu.VMEM)
    return pl.pallas_call(
        assemble_body,
        in_specs=[pl.BlockSpec(memory_space=pltpu.SMEM)] + [vmem] * len(parts),
        out_specs=vmem,
        out_shape=jax.ShapeDtypeStruct((count, rows * len(parts), width), parts[0].dtype),
        compiler_params=pltpu.CompilerParams(vmem_limit_bytes=24 << 20),
        name="assemble",
    )(places, *parts)


def start_weight(projector_weight, dp_index, dp_count):
    width_part, features = projector_weight.shape
    rows = width_part // dp_count
    mp_count = lax.axis_size(MP)
    own = lax.dynamic_slice(projector_weight, (dp_index * rows, 0), (rows, features))
    own = own.reshape(rows, mp_count, features // mp_count).transpose(1, 0, 2)
    return lax.all_to_all(own, MP, split_axis=0, concat_axis=0, tiled=True)


def gather_weight(own, plane, core):
    parts, places = [], []
    for step in range(RING):
        piece = own if step == 0 else shift(own, "dp_0", step)
        source = (plane - step) % RING * 2
        parts += [piece, swap(piece)]
        places += [source + core, source + 1 - core]
    places = jnp.stack(places).astype(jnp.int32)
    return assemble(parts, places)


def ring(own, axis):
    half = own.shape[0] // 2
    left = shift(own, axis, 1)
    right = shift(own, axis, -1)
    low = shift(left[:half], axis, 1)
    high = shift(right[half:], axis, -1)
    return left, right, jnp.concatenate([low, high])


OWN, LEFT, RIGHT, FAR = 0, -1, 1, 2


def plane_gather(own, first_axis, second_axis):
    left, right, far = ring(own, first_axis)
    row = {OWN: own, LEFT: left, RIGHT: right, FAR: far}
    pieces = {(OWN, early): x for early, x in row.items()}
    for early in (OWN, LEFT, RIGHT, FAR):
        pieces[LEFT, early] = shift(row[early], second_axis, 1)
    for early in (OWN, RIGHT, LEFT, FAR):
        pieces[RIGHT, early] = shift(row[early], second_axis, -1)
    for late, early, step in ((LEFT, OWN, 1), (LEFT, LEFT, 1), (RIGHT, RIGHT, -1), (RIGHT, FAR, -1)):
        pieces[FAR, early] = shift(pieces[late, early], second_axis, step)
    return pieces


def block_table(keys, x_first):
    y = lax.axis_index("mp_0")
    x = lax.axis_index("mp_1")
    table = []
    for late, early in keys:
        dy, dx = (late, early) if x_first else (early, late)
        table.append((y + dy) % RING * RING + (x + dx) % RING)
    return jnp.stack(table).astype(jnp.int32)


def products(parts, weight, table, base, out, first, unroll=False):
    rows, width = base.shape if base is not None else out.shape
    tall, wide = rows // 2, width // 2

    def tile(t, carry):
        i = pl.multiple_of(t // 2 * tall, tall)
        j = pl.multiple_of(t % 2 * wide, wide)
        value = None if base is None else base[pl.ds(i, tall), pl.ds(j, wide)]
        for spot, part in enumerate(parts):
            piece = jnp.dot(
                part[pl.ds(i, tall), :],
                weight[table[spot], :, pl.ds(j, wide)],
                preferred_element_type=jnp.float32,
            )
            value = piece if value is None else value + piece
        out[pl.ds(pl.multiple_of(first + i, tall), tall), pl.ds(j, wide)] = value
        return carry

    lax.fori_loop(0, 4, tile, 0, unroll=unroll)


def matmul_body(n, has_base, table, *refs):
    products(refs[:n], refs[n], table, refs[n + 1] if has_base else None, refs[-1], 0)


def matmul(parts, weight, table, base=None):
    rows, depth = parts[0].shape
    width = weight.shape[2]
    count = len(parts)
    operands = list(parts) + [weight] + ([] if base is None else [base])
    vmem = pl.BlockSpec(memory_space=pltpu.VMEM)
    return pl.pallas_call(
        lambda *refs: matmul_body(len(parts), base is not None, *refs),
        in_specs=[pl.BlockSpec(memory_space=pltpu.SMEM)] + [vmem] * len(operands),
        out_specs=vmem,
        out_shape=jax.ShapeDtypeStruct((rows, width), jnp.float32),
        cost_estimate=pl.CostEstimate(
            flops=2 * count * rows * depth * width,
            transcendentals=0,
            bytes_accessed=2 * count * depth * (rows + width) + 4 * rows * width,
        ),
        compiler_params=pltpu.CompilerParams(vmem_limit_bytes=24 << 20),
        name="embed",
    )(table, *operands)


ALL = (OWN, LEFT, RIGHT, FAR)
STEPS = (
    [(OWN, early) for early in ALL],
    [(late, early) for late in (LEFT, RIGHT) for early in ALL],
    [(FAR, OWN), (FAR, RIGHT)],
)
LAST = [(FAR, LEFT), (FAR, FAR)]


def embed(pieces, weight, x_first):
    value = None
    for keys in STEPS:
        table = block_table(keys, x_first)
        value = matmul([pieces[key] for key in keys], weight, table, value)
    return value


def finish_body(n, local_rows, *refs):
    tables, places, weight, bases = refs[:2], refs[2], refs[3], refs[4:6]
    parts = refs[6 : 6 + n], refs[6 + n : 6 + 2 * n]
    owned, keep, send, by_y, by_x, variance, values, rows = refs[6 + 2 * n :]
    count, width = values.shape
    mean = jnp.zeros((1, width), jnp.float32)
    for h in range(2):
        products(parts[h], weight, tables[h], bases[h], values, h * (count // 2), True)
    for start in range(0, count, local_rows):
        value = values[start : start + local_rows, :]
        mean = mean + jnp.sum(value, axis=0, keepdims=True)
        at = start // local_rows
        owned[places[at]] = value
        back = (0, 3, 1, 2)[at // 2]
        out = send if at % 2 else keep
        out[back] = value.astype(out.dtype)
    mean = mean / count
    square = jnp.zeros_like(mean)
    for start in range(0, count, local_rows):
        centered = values[start : start + local_rows, :] - mean
        square = square + jnp.sum(centered * centered, axis=0, keepdims=True)
        rows[start : start + local_rows, :] = centered.astype(rows.dtype)
    variance[...] = square / (count - 1)
    blocks = count // GRAM_BLOCK
    half = by_y.shape[2]
    per = 2 * half // GRAM_BLOCK

    def store(at, block):
        owner, first = at // per, at % per * GRAM_BLOCK
        y, x = owner // RING, owner % RING
        split = min(max(half - first, 0), GRAM_BLOCK)
        if split:
            by_y[y, x, first : first + split, :] = block[:split]
        if split < GRAM_BLOCK:
            low = first + split - half
            by_x[x, y, low : low + GRAM_BLOCK - split, :] = block[split:]

    spot = blocks
    strip_rows = 2 * GRAM_BLOCK
    for i in range(0, blocks, 2):
        strip = lax.dot_general(
            rows[i * GRAM_BLOCK : i * GRAM_BLOCK + strip_rows, :],
            rows[i * GRAM_BLOCK :, :],
            (((1,), (1,)), ((), ())),
            preferred_element_type=jnp.float32,
        ).astype(by_y.dtype)
        for r in range(2):
            for k in range(i + r, blocks):
                at = i + r if k == i + r else spot
                spot += k != i + r
                store(
                    at,
                    strip[
                        r * GRAM_BLOCK : (r + 1) * GRAM_BLOCK,
                        (k - i) * GRAM_BLOCK : (k - i + 1) * GRAM_BLOCK,
                    ],
                )
    while spot < per * RING * RING:
        store(spot, jnp.zeros((GRAM_BLOCK, GRAM_BLOCK), by_y.dtype))
        spot += 1


def finish(tops, weight, bases, places):
    count = sum(base.shape[0] for base in bases)
    width = bases[0].shape[1]
    local_rows = count // places.shape[0]
    n = count // GRAM_BLOCK
    per = -(-(n * (n + 1) // 2) // (RING * RING))
    half = jax.ShapeDtypeStruct((RING, RING, per * GRAM_BLOCK // 2, GRAM_BLOCK), jnp.bfloat16)
    back = jax.ShapeDtypeStruct((RING, local_rows, width), jnp.bfloat16)
    tables = [block_table(LAST, x_first) for x_first in (True, False)]
    operands = [weight, *bases] + [pieces[key] for pieces in tops for key in LAST]
    smem = pl.BlockSpec(memory_space=pltpu.SMEM)
    vmem = pl.BlockSpec(memory_space=pltpu.VMEM)
    return pl.pallas_call(
        lambda *refs: finish_body(len(LAST), local_rows, *refs),
        in_specs=[smem] * 3 + [vmem] * len(operands),
        out_specs=[vmem] * 6,
        out_shape=(
            jax.ShapeDtypeStruct((count // local_rows, local_rows, width), jnp.float32),
            back,
            back,
            half,
            half,
            jax.ShapeDtypeStruct((1, width), jnp.float32),
        ),
        scratch_shapes=[
            pltpu.VMEM((count, width), jnp.float32),
            pltpu.VMEM((count, width), jnp.bfloat16),
        ],
        cost_estimate=pl.CostEstimate(
            flops=2 * count * count * width, transcendentals=0, bytes_accessed=8 * count * width
        ),
        compiler_params=pltpu.CompilerParams(vmem_limit_bytes=40 << 20),
        name="finish",
    )(*tables, places, *operands)


def scatter(x, axis):
    at = lax.axis_index(axis)
    blocks = [lax.dynamic_index_in_dim(x, at, 0, keepdims=False)]
    for step in (1, 3, 2):
        piece = lax.dynamic_index_in_dim(x, (at + step) % RING, 0, keepdims=False)
        blocks.append(shift(piece, axis, step))
    return blocks


def add(blocks):
    return sum(block.astype(jnp.float32) for block in blocks)


def score_body(place, invariance, variance, *refs):
    parts, out = refs[:-1], refs[-1]
    count = len(parts) // 2
    half = parts[0].shape[0]
    diagonal = place[1]
    value = jnp.zeros((8, GRAM_BLOCK), jnp.float32)
    for h in range(2):
        block = add([part[...] for part in parts[h * count : (h + 1) * count]])
        row = lax.broadcasted_iota(jnp.int32, block.shape, 0) + (2 * place[0] + h) * half
        block = block * block * jnp.where(row < diagonal, 1.0, 2.0)
        value = value + jnp.sum(block.reshape(half // 8, 8, GRAM_BLOCK), axis=0)
    frobenius = jnp.sum(value) / ((diagonal - 1) * (diagonal - 1)).astype(jnp.float32)
    spread = variance[...]
    hinge = jnp.sum(jnp.maximum(1.0 - jnp.sqrt(spread + epsilon), 0.0))
    off = frobenius - jnp.sum(spread * spread)
    lane = lax.broadcasted_iota(jnp.int32, out.shape, 1)
    row = jnp.where(lane == 0, invariance[0, 0], jnp.where(lane == 1, hinge, off))
    out[...] = jnp.where(lane < 3, row, 0.0)


def score(place, invariance, variance, by_y, by_x):
    smem = pl.BlockSpec(memory_space=pltpu.SMEM)
    vmem = pl.BlockSpec(memory_space=pltpu.VMEM)
    parts = by_y + by_x
    return pl.pallas_call(
        score_body,
        in_specs=[smem] * 2 + [vmem] * (1 + len(parts)),
        out_specs=vmem,
        out_shape=jax.ShapeDtypeStruct((lax.axis_size(AXES), 128), jnp.float32),
        compiler_params=pltpu.CompilerParams(vmem_limit_bytes=16 << 20),
        name="score",
    )(place, invariance, variance, *parts)


def terms_body(scales, rows, out):
    sums = jnp.sum(rows[...], axis=0, keepdims=True)
    lane = lax.broadcasted_iota(jnp.int32, sums.shape, 1)
    losses = [jnp.sum(jnp.where(lane == n, sums, 0.0)) * scales[n] for n in range(3)]
    for n in range(3):
        out[n] = losses[n]
    out[3] = 25.0 * losses[0] + 25.0 * losses[1] + losses[2]


def loss_terms(rows, scales):
    rows = lax.all_to_all(rows, AXES, split_axis=0, concat_axis=0, tiled=True)
    smem = pl.BlockSpec(memory_space=pltpu.SMEM)
    return pl.pallas_call(
        terms_body,
        in_specs=[smem, pl.BlockSpec(memory_space=pltpu.VMEM)],
        out_specs=smem,
        out_shape=jax.ShapeDtypeStruct((4,), jnp.float32),
        compiler_params=pltpu.CompilerParams(vmem_limit_bytes=4 << 20),
        name="terms",
    )(jnp.array(scales, jnp.float32), rows)


def distances_body(anchors, images, *refs):
    parts, out, aligned = refs[:-2], refs[-2], refs[-1]
    count, size, width = aligned.shape

    for n, part in enumerate(parts):
        for k in range(2):
            at = 2 * n + k
            wanted = lax.broadcasted_iota(jnp.int32, (size, size), 0)
            onehot = jnp.where(wanted == images[at : at + 1, :], 1.0, 0.0).astype(part.dtype)
            aligned[at] = jnp.dot(onehot, part[k], preferred_element_type=jnp.float32)

    def step(at, value):
        for anchor in range(2):
            differ = aligned[at] - aligned[anchors[anchor]]
            value = value + jnp.sum((differ * differ).reshape(size // 8, 8, width), axis=0)
        return value

    value = lax.fori_loop(0, count, step, jnp.zeros((8, width), jnp.float32))
    out[0, 0] = jnp.sum(value)


def distances(anchors, images, parts):
    count, size = images.shape
    width = parts[0].shape[2]
    smem = pl.BlockSpec(memory_space=pltpu.SMEM)
    vmem = pl.BlockSpec(memory_space=pltpu.VMEM)
    value = pl.pallas_call(
        distances_body,
        in_specs=[smem] + [vmem] * (1 + len(parts)),
        out_specs=smem,
        out_shape=jax.ShapeDtypeStruct((1, 1), jnp.float32),
        scratch_shapes=[pltpu.VMEM((count, size, width), jnp.float32)],
        cost_estimate=pl.CostEstimate(
            flops=2 * count * size * size * width,
            transcendentals=0,
            bytes_accessed=2 * count * size * width,
        ),
        compiler_params=pltpu.CompilerParams(vmem_limit_bytes=16 << 20),
        name="distances",
    )(anchors, images, *parts)
    return value


def exchange(keep, send):
    swapped = swap(send)
    pairs = [jnp.stack([keep[dz], swapped[dz]]) for dz in range(RING)]
    return [pairs[dz] if dz == 0 else shift(pairs[dz], "dp_0", dz) for dz in range(RING)]


def local(crop_hidden, projector_weight, pairing):
    crop_count, local_rows, width_part = crop_hidden.shape
    features = projector_weight.shape[1]
    dp_count = lax.axis_size(DP)
    dp_index = lax.axis_index(DP)
    plane = lax.axis_index("dp_0")
    core = lax.axis_index("dp_1")
    batch_rows = local_rows * dp_count

    def crop_of(dz, dc):
        return (plane + dz) % RING * 2 + (core ^ dc)

    picked = [
        jnp.stack(
            [lax.dynamic_index_in_dim(crop_hidden, crop_of(dz, dc), 0, keepdims=False) for dz in range(RING)]
        )
        for dc in range(2)
    ]
    hidden = exchange(*picked)
    hidden = [part.reshape(2 * local_rows, width_part) for part in hidden]
    weight = gather_weight(start_weight(projector_weight, dp_index, dp_count), plane, core)
    feature_part = weight.shape[2]
    tops = (
        plane_gather(jnp.concatenate(hidden[:2]), "mp_1", "mp_0"),
        plane_gather(jnp.concatenate([hidden[3], hidden[2]]), "mp_0", "mp_1"),
    )
    bases = [embed(pieces, weight, x_first) for pieces, x_first in zip(tops, (True, False))]
    sources = [(dz, dc) for dz in (0, 1, 3, 2) for dc in range(2)]
    places = jnp.stack([(plane - dz) % RING * 2 + (core ^ dc) for dz, dc in sources])
    owned, keep, send, by_y, by_x, variance = finish(tops, weight, bases, places.astype(jnp.int32))
    by_y = add(scatter(by_y, "mp_0")).astype(jnp.bfloat16)
    by_x = add(scatter(by_x, "mp_1")).astype(jnp.bfloat16)
    by_y = scatter(by_y, "mp_1")
    by_x = scatter(by_x, "mp_0")

    owned = owned.reshape(batch_rows, feature_part).T[:, None, :]

    back = exchange(keep, send)
    turned = jnp.concatenate(
        [
            lax.dynamic_index_in_dim(pairing, crop_of(-dz, dc), 0, keepdims=True)
            for dz in range(RING)
            for dc in range(2)
        ],
        axis=0,
    )
    anchors = jnp.stack([plane * 2 + (core ^ anchor) for anchor in range(2)]).astype(jnp.int32)
    invariance = distances(anchors, turned, back)

    place = jnp.stack([lax.axis_index(MP), jnp.int32(batch_rows)]).astype(jnp.int32)
    rows = score(place, invariance, variance, by_y, by_x)
    scales = (
        1.0 / (2 * (crop_count - 1) * batch_rows * features),
        1.0 / (crop_count * features),
        1.0 / (crop_count * features),
    )
    return (owned, loss_terms(rows, scales))


def solution(mesh):
    torus = Mesh(mesh.devices.reshape(4, 2, 4, 4), ("dp_0", "dp_1", "mp_0", "mp_1"))
    placed = (P(None, DP, MP), P(MP, None), P(None, DP))
    return jax.shard_map(
        local, mesh=torus, in_specs=placed, out_specs=(P(MP, DP, None), P()), check_vma=False
    )
```

profile of v0, /device:TPU:0, one launch (start us, length us, event | category | flops | bytes accessed | tf_op | source)
XLA Modules:
  0.0 369.6 jit_solution(18411765128107487184)
XLA Ops:
  4.9 4.2 %collective-permute-start.23 = (bf16[2,192,512]{2,1,0:T(8,128)(2,1)S(1)}, bf16[2,192,512]{2,1,0:T(8,128)(2,1)}, u32[]{:S(2)}, u32[]{:S(2)}) collective-permute-start(bf16[2,192,512]{2,1,0:T(8,128)(2,1)S(1)} %pad_maximum_fusion.5), channel_id=1, source_target_pairs={{0,96},{32,0},{64,32},{96,64},{1,97},{33,1},{65,33},{97,65},{2,98}... | collective-permute-start | bytes 1179656 | tf_op jit(solution)/shard_map/ppermute | solution.py:20
  10.6 15.6 %collective-permute-done.23 = bf16[2,192,512]{2,1,0:T(8,128)(2,1)} collective-permute-done((bf16[2,192,512]{2,1,0:T(8,128)(2,1)S(1)}, bf16[2,192,512]{2,1,0:T(8,128)(2,1)}, u32[]{:S(2)}, u32[]{:S(2)}) %collective-permute-start.23) | collective-permute-done | bytes 393248 | tf_op jit(solution)/shard_map/ppermute | solution.py:20
  33.8 5.8 %all-to-all-start = ((bf16[16,64,512]{2,1,0:T(8,128)(2,1)}), bf16[16,64,512]{2,1,0:T(8,128)(2,1)S(1)}, u32[]{:S(2)}, u32[]{:S(2)}) async-start(bf16[16,64,512]{2,1,0:T(8,128)(2,1)} %bitcast.86), calls=%async_computation | async-start | bytes 2097152 | tf_op jit(solution)/shard_map/all_to_all | solution.py:59
  43.8 13.0 %collective-permute-done.30.refs_2_ = bf16[768,512]{1,0:T(8,128)(2,1)} collective-permute-done((bf16[768,512]{1,0:T(8,128)(2,1)S(1)}, bf16[768,512]{1,0:T(8,128)(2,1)}, u32[]{:S(2)}, u32[]{:S(2)}) %collective-permute-start.30) | collective-permute-done | bytes 786464 | tf_op jit(solution)/shard_map/ppermute | solution.py:20
  56.7 3.5 collective-permute-start.11
  62.6 8.0 %collective-permute-done.25.refs_1_ = bf16[768,512]{1,0:T(8,128)(2,1)} collective-permute-done((bf16[768,512]{1,0:T(8,128)(2,1)S(1)}, bf16[768,512]{1,0:T(8,128)(2,1)}, u32[]{:S(2)}, u32[]{:S(2)}) %collective-permute-start.25) | collective-permute-done | bytes 786464 | tf_op jit(solution)/shard_map/ppermute | solution.py:20
  72.3 3.5 collective-permute-start.3
  75.9 11.2 %collective-permute-done.14.refs_2_ = bf16[768,512]{1,0:T(8,128)(2,1)} collective-permute-done((bf16[768,512]{1,0:T(8,128)(2,1)S(1)}, bf16[768,512]{1,0:T(8,128)(2,1)}, u32[]{:S(2)}, u32[]{:S(2)}) %collective-permute-start.14) | collective-permute-done | bytes 786464 | tf_op jit(solution)/shard_map/ppermute | solution.py:20
  87.0 3.8 %collective-permute-start.5 = (bf16[16,64,512]{2,1,0:T(8,128)(2,1)S(1)}, bf16[16,64,512]{2,1,0:T(8,128)(2,1)}, u32[]{:S(2)}, u32[]{:S(2)}) collective-permute-start(bf16[16,64,512]{2,1,0:T(8,128)(2,1)S(1)} %all-to-all-done.refs_0_), channel_id=1, source_target_pairs={{0,96},{32,0},{64,32},{96,64},{1,97},{33,1},{65,33},{97,65},{2,98}... | collective-permute-start | bytes 3145736 | tf_op jit(solution)/shard_map/ppermute | solution.py:20
  94.4 17.7 %collective-permute-done.9.refs_1_ = bf16[768,512]{1,0:T(8,128)(2,1)} collective-permute-done((bf16[768,512]{1,0:T(8,128)(2,1)S(1)}, bf16[768,512]{1,0:T(8,128)(2,1)}, u32[]{:S(2)}, u32[]{:S(2)}) %collective-permute-start.9) | collective-permute-done | bytes 786464 | tf_op jit(solution)/shard_map/ppermute | solution.py:20
  115.4 5.4 %collective-permute-done.3.refs_4_ = bf16[16,64,512]{2,1,0:T(8,128)(2,1)} collective-permute-done((bf16[16,64,512]{2,1,0:T(8,128)(2,1)S(1)}, bf16[16,64,512]{2,1,0:T(8,128)(2,1)}, u32[]{:S(2)}, u32[]{:S(2)}) %collective-permute-start.3) | collective-permute-done | bytes 1048608 | tf_op jit(solution)/shard_map/ppermute | solution.py:20
  129.2 36.2 %collective-permute-done.17 = bf16[384,512]{1,0:T(8,128)(2,1)} collective-permute-done((bf16[384,512]{1,0:T(8,128)(2,1)S(1)}, bf16[384,512]{1,0:T(8,128)(2,1)}, u32[]{:S(2)}, u32[]{:S(2)}) %collective-permute-start.17) | collective-permute-done | bytes 393248 | tf_op jit(solution)/shard_map/ppermute | solution.py:20
  171.9 10.8 %collective-permute-done.37.refs_6_ = bf16[768,512]{1,0:T(8,128)(2,1)S(1)} collective-permute-done((bf16[768,512]{1,0:T(8,128)(2,1)}, bf16[768,512]{1,0:T(8,128)(2,1)S(1)}, u32[]{:S(2)}, u32[]{:S(2)}) %collective-permute-start.37) | collective-permute-done | bytes 786464 | tf_op jit(solution)/shard_map/ppermute | solution.py:20
  185.4 6.7 %collective-permute-done.15.refs_2_ = bf16[768,512]{1,0:T(8,128)(2,1)} collective-permute-done((bf16[768,512]{1,0:T(8,128)(2,1)}, bf16[768,512]{1,0:T(8,128)(2,1)}, u32[]{:S(2)}, u32[]{:S(2)}) %collective-permute-start.15) | collective-permute-done | bytes 786464 | tf_op jit(solution)/shard_map/ppermute | solution.py:20
  192.1 12.5 %collective-permute-done.16.refs_3_ = bf16[768,512]{1,0:T(8,128)(2,1)S(1)} collective-permute-done((bf16[768,512]{1,0:T(8,128)(2,1)}, bf16[768,512]{1,0:T(8,128)(2,1)S(1)}, u32[]{:S(2)}, u32[]{:S(2)}) %collective-permute-start.16) | collective-permute-done | bytes 786464 | tf_op jit(solution)/shard_map/ppermute | solution.py:20
  207.6 14.8 %collective-permute-done.10.refs_1_ = bf16[768,512]{1,0:T(8,128)(2,1)} collective-permute-done((bf16[768,512]{1,0:T(8,128)(2,1)}, bf16[768,512]{1,0:T(8,128)(2,1)}, u32[]{:S(2)}, u32[]{:S(2)}) %collective-permute-start.10) | collective-permute-done | bytes 786464 | tf_op jit(solution)/shard_map/ppermute | solution.py:20
  228.6 3.7 %assemble.1.refs_5_.refs_9_.refs_3_ = bf16[16,512,512]{2,1,0:T(8,128)(2,1)S(1)} custom-call(s32[8]{0:T(128)S(1)} %stack.202.places, bf16[16,64,512]{2,1,0:T(8,128)(2,1)S(1)} %all-to-all-done.refs_0_, bf16[16,64,512]{2,1,0:T(8,128)(2,1)S(1)} %copy-done.5, bf16[16,64,512]{2,1,0:T(8,128)(2,1)} %collective-permute-done.1.refs_2_, ...), custom_call_target="tpu_custom_call" | custom-call | tf_op jit(solution)/shard_map/assemble/pallas_call | solution.py:43
  232.4 4.9 %embed.9.refs_10_ = f32[768,512]{1,0:T(8,128)S(1)} custom-call(s32[4]{0:T(128)S(1)} %pad_add_fusion.5.refs_0_, bf16[768,512]{1,0:T(8,128)(2,1)S(1)} %pad_maximum_fusion.2.refs_1_, bf16[768,512]{1,0:T(8,128)(2,1)} %collective-permute-done.30.refs_2_, bf16[768,512]{1,0:T(8,128)(2,1)} %collective-permute-done.27.refs_3_, ...), custom_call_target="tpu_custom_call" | custom-call | flops 1610612736 | bytes 6815744 | tf_op jit(solution)/shard_map/embed/pallas_call | solution.py:139
  239.4 3.5 collective-permute-done.38.refs_8_
  245.1 3.6 collective-permute-start.42
  248.6 11.2 %collective-permute-done.29.refs_2_ = bf16[768,512]{1,0:T(8,128)(2,1)S(1)} collective-permute-done((bf16[768,512]{1,0:T(8,128)(2,1)}, bf16[768,512]{1,0:T(8,128)(2,1)S(1)}, u32[]{:S(2)}, u32[]{:S(2)}) %collective-permute-start.29) | collective-permute-done | bytes 786464 | tf_op jit(solution)/shard_map/ppermute | solution.py:20
  259.9 3.7 embed.6.refs_10_
  263.6 5.9 %embed.10.refs_4_ = f32[768,512]{1,0:T(8,128)S(1)} custom-call(s32[8]{0:T(128)S(1)} %stack.225.refs_0_, bf16[768,512]{1,0:T(8,128)(2,1)} %collective-permute-done.25.refs_1_, bf16[768,512]{1,0:T(8,128)(2,1)} %collective-permute-done.31.refs_2_, bf16[768,512]{1,0:T(8,128)(2,1)S(1)} %copy-done.7, bf16[768,512]{1,0:T(8,128)(2,1)S(1)} %collective-permute-done.35.refs_4_, ...), custom_call_target="tpu_custom_call" | custom-call | flops 3221225472 | bytes 12058624 | tf_op jit(solution)/shard_map/embed/pallas_call | solution.py:139
  269.5 6.1 %embed.7.refs_4_ = f32[768,512]{1,0:T(8,128)S(1)} custom-call(s32[8]{0:T(128)S(1)} %stack.216.refs_0_, bf16[768,512]{1,0:T(8,128)(2,1)} %collective-permute-done.9.refs_1_, bf16[768,512]{1,0:T(8,128)(2,1)} %collective-permute-done.15.refs_2_, bf16[768,512]{1,0:T(8,128)(2,1)S(1)} %copy-done.11, bf16[768,512]{1,0:T(8,128)(2,1)S(1)} %collective-permute-done.19.refs_4_, ...), custom_call_target="tpu_custom_call" | custom-call | flops 3221225472 | bytes 12058624 | tf_op jit(solution)/shard_map/embed/pallas_call | solution.py:139
  280.4 7.6 %finish.1 = (f32[8,192,512]{2,1,0:T(8,128)S(1)}, bf16[4,192,512]{2,1,0:T(8,128)(2,1)S(1)}, bf16[4,192,512]{2,1,0:T(8,128)(2,1)}, bf16[4,4,320,128]{3,2,1,0:T(8,1...) custom-call(s32[2]{0:T(128)S(1)} %get-tuple-element.56.refs_0_, ...), custom_call_target="tpu_custom_call" | custom-call | flops 2415919104 | bytes 6291456 | tf_op jit(solution)/shard_map/finish/pallas_call | solution.py:245
  292.5 3.7 collective-permute-start.54
  299.8 4.7 %collective-permute-done.53 = bf16[4,320,128]{2,1,0:T(8,128)(2,1)S(1)} collective-permute-done((bf16[4,320,128]{2,1,0:T(8,128)(2,1)S(1)}, bf16[4,320,128]{2,1,0:T(8,128)(2,1)S(1)}, u32[]{:S(2)}, u32[]{:S(2)}) %collective-permute-start.53) | collective-permute-done | bytes 327712 | tf_op jit(solution)/shard_map/ppermute | solution.py:20
  304.5 6.4 %collective-permute-done.54 = bf16[4,320,128]{2,1,0:T(8,128)(2,1)S(1)} collective-permute-done((bf16[4,320,128]{2,1,0:T(8,128)(2,1)S(1)}, bf16[4,320,128]{2,1,0:T(8,128)(2,1)S(1)}, u32[]{:S(2)}, u32[]{:S(2)}) %collective-permute-start.54) | collective-permute-done | bytes 327712 | tf_op jit(solution)/shard_map/ppermute | solution.py:20
  315.2 6.1 %collective-permute-start.46 = (bf16[2,192,512]{2,1,0:T(8,128)(2,1)S(1)}, bf16[2,192,512]{2,1,0:T(8,128)(2,1)S(1)}, u32[]{:S(2)}, u32[]{:S(2)}) collective-permute-start(bf16[2,192,512]{2,1,0:T(8,128)(2,1)S(1)} %pad_maximum_fusion.10), channel_id=1, source_target_pairs={{0,96},{32,0},{64,32},{96,64},{1,97},{33,1},{65,33},{97,65},{2,98}... | collective-permute-start | bytes 1179656 | tf_op jit(solution)/shard_map/ppermute | solution.py:20
  329.0 8.9 %collective-permute-done.46.refs_3_ = bf16[2,192,512]{2,1,0:T(8,128)(2,1)S(1)} collective-permute-done((bf16[2,192,512]{2,1,0:T(8,128)(2,1)S(1)}, bf16[2,192,512]{2,1,0:T(8,128)(2,1)S(1)}, u32[]{:S(2)}, u32[]{:S(2)}) %collective-permute-start.46) | collective-permute-done | bytes 393248 | tf_op jit(solution)/shard_map/ppermute | solution.py:20
  349.6 9.0 %all-to-all-start.1 = ((f32[128,1,128]{2,1,0:T(1,128)}), f32[128,1,128]{2,1,0:T(1,128)S(1)}, u32[]{:S(2)}, u32[]{:S(2)}) async-start(f32[128,1,128]{2,1,0:T(1,128)} %bitcast.55), calls=%async_computation.1 | async-start | bytes 131072 | tf_op jit(solution)/shard_map/all_to_all | solution.py:326
  361.0 5.7 %broadcast_in_dim.3 = f32[512,1,1536]{2,1,0:T(1,128)} reshape(f32[512,1536]{1,0:T(8,128)} %bitcast.84) | data formatting | bytes 6291456 | tf_op jit(solution)/shard_map/broadcast_in_dim | solution.py:422
  (188 shorter events, 100.9 us)
Async XLA Ops:
  9.3 33.7 %collective-permute-start.8 = (bf16[2,192,512]{2,1,0:T(8,128)(2,1)S(1)}, bf16[2,192,512]{2,1,0:T(8,128)(2,1)S(1)}, u32[]{:S(2)}, u32[]{:S(2)}) collective-permute-start(bf16[2,192,512]{2,1,0:T(8,128)(2,1)S(1)} %pad_maximum_fusion.4), channel_id=1, source_target_pairs={{0,32},{32,64},{64,96},{96,0},{1,33},{33,65},{65,97},{97,1},{2,34}... | collective-permute-start | bytes 1179656 | tf_op jit(solution)/shard_map/ppermute | solution.py:20
  28.1 28.6 %collective-permute-start.30 = (bf16[768,512]{1,0:T(8,128)(2,1)S(1)}, bf16[768,512]{1,0:T(8,128)(2,1)}, u32[]{:S(2)}, u32[]{:S(2)}) collective-permute-start(bf16[768,512]{1,0:T(8,128)(2,1)S(1)} %pad_maximum_fusion.2.refs_1_), channel_id=1, source_target_pairs={{0,4},{4,8},{8,12},{12,0},{1,5},{5,9},{9,13},{13,1},{2,6},{6,10},{... | collective-permute-start | bytes 2359304 | tf_op jit(solution)/shard_map/ppermute | solution.py:20
  29.8 30.4 %collective-permute-start.27 = (bf16[768,512]{1,0:T(8,128)(2,1)S(1)}, bf16[768,512]{1,0:T(8,128)(2,1)}, u32[]{:S(2)}, u32[]{:S(2)}) collective-permute-start(bf16[768,512]{1,0:T(8,128)(2,1)S(1)} %pad_maximum_fusion.2.refs_1_), channel_id=1, source_target_pairs={{0,12},{4,0},{8,4},{12,8},{1,13},{5,1},{9,5},{13,9},{2,14},{6,2},{... | collective-permute-start | bytes 2359304 | tf_op jit(solution)/shard_map/ppermute | solution.py:20
  33.8 28.8 %all-to-all-start = ((bf16[16,64,512]{2,1,0:T(8,128)(2,1)}), bf16[16,64,512]{2,1,0:T(8,128)(2,1)S(1)}, u32[]{:S(2)}, u32[]{:S(2)}) async-start(bf16[16,64,512]{2,1,0:T(8,128)(2,1)} %bitcast.86), calls=%async_computation | async-start | bytes 2097152 | tf_op jit(solution)/shard_map/all_to_all | solution.py:59
  39.6 31.0 %collective-permute-start.25 = (bf16[768,512]{1,0:T(8,128)(2,1)S(1)}, bf16[768,512]{1,0:T(8,128)(2,1)}, u32[]{:S(2)}, u32[]{:S(2)}) collective-permute-start(bf16[768,512]{1,0:T(8,128)(2,1)S(1)} %pad_maximum_fusion.2.refs_1_), channel_id=1, source_target_pairs={{0,1},{1,2},{2,3},{3,0},{4,5},{5,6},{6,7},{7,4},{8,9},{9,10},{10,1... | collective-permute-start | bytes 2359304 | tf_op jit(solution)/shard_map/ppermute | solution.py:20
  41.6 30.8 %collective-permute-start.36 = (bf16[768,512]{1,0:T(8,128)(2,1)S(1)}, bf16[768,512]{1,0:T(8,128)(2,1)}, u32[]{:S(2)}, u32[]{:S(2)}) collective-permute-start(bf16[768,512]{1,0:T(8,128)(2,1)S(1)} %pad_maximum_fusion.2.refs_1_), channel_id=1, source_target_pairs={{0,3},{1,0},{2,1},{3,2},{4,7},{5,4},{6,5},{7,6},{8,11},{9,8},{10,9... | collective-permute-start | bytes 2359304 | tf_op jit(solution)/shard_map/ppermute | solution.py:20
  43.1 44.0 %collective-permute-start.14 = (bf16[768,512]{1,0:T(8,128)(2,1)S(1)}, bf16[768,512]{1,0:T(8,128)(2,1)}, u32[]{:S(2)}, u32[]{:S(2)}) collective-permute-start(bf16[768,512]{1,0:T(8,128)(2,1)S(1)} %pad_maximum_fusion.1.refs_1_), channel_id=1, source_target_pairs={{0,1},{1,2},{2,3},{3,0},{4,5},{5,6},{6,7},{7,4},{8,9},{9,10},{10,1... | collective-permute-start | bytes 2359304 | tf_op jit(solution)/shard_map/ppermute | solution.py:20
  56.7 34.1 %collective-permute-start.11 = (bf16[768,512]{1,0:T(8,128)(2,1)S(1)}, bf16[768,512]{1,0:T(8,128)(2,1)}, u32[]{:S(2)}, u32[]{:S(2)}) collective-permute-start(bf16[768,512]{1,0:T(8,128)(2,1)S(1)} %pad_maximum_fusion.1.refs_1_), channel_id=1, source_target_pairs={{0,3},{1,0},{2,1},{3,2},{4,7},{5,4},{6,5},{7,6},{8,11},{9,8},{10,9... | collective-permute-start | bytes 2359304 | tf_op jit(solution)/shard_map/ppermute | solution.py:20
  60.2 30.7 %collective-permute-start.20 = (bf16[768,512]{1,0:T(8,128)(2,1)S(1)}, bf16[768,512]{1,0:T(8,128)(2,1)}, u32[]{:S(2)}, u32[]{:S(2)}) collective-permute-start(bf16[768,512]{1,0:T(8,128)(2,1)S(1)} %pad_maximum_fusion.1.refs_1_), channel_id=1, source_target_pairs={{0,12},{4,0},{8,4},{12,8},{1,13},{5,1},{9,5},{13,9},{2,14},{6,2},{... | collective-permute-start | bytes 2359304 | tf_op jit(solution)/shard_map/ppermute | solution.py:20
  70.6 41.8 %collective-permute-start.1 = (bf16[16,64,512]{2,1,0:T(8,128)(2,1)S(1)}, bf16[16,64,512]{2,1,0:T(8,128)(2,1)}, u32[]{:S(2)}, u32[]{:S(2)}) collective-permute-start(bf16[16,64,512]{2,1,0:T(8,128)(2,1)S(1)} %all-to-all-done.refs_0_), channel_id=1, source_target_pairs={{0,32},{32,64},{64,96},{96,0},{1,33},{33,65},{65,97},{97,1},{2,34}... | collective-permute-start | bytes 3145736 | tf_op jit(solution)/shard_map/ppermute | solution.py:20
  72.3 48.4 %collective-permute-start.3 = (bf16[16,64,512]{2,1,0:T(8,128)(2,1)S(1)}, bf16[16,64,512]{2,1,0:T(8,128)(2,1)}, u32[]{:S(2)}, u32[]{:S(2)}) collective-permute-start(bf16[16,64,512]{2,1,0:T(8,128)(2,1)S(1)} %all-to-all-done.refs_0_), channel_id=1, source_target_pairs={{0,64},{32,96},{64,0},{96,32},{1,65},{33,97},{65,1},{97,33},{2,66}... | collective-permute-start | bytes 3145736 | tf_op jit(solution)/shard_map/ppermute | solution.py:20
  87.0 33.7 %collective-permute-start.5 = (bf16[16,64,512]{2,1,0:T(8,128)(2,1)S(1)}, bf16[16,64,512]{2,1,0:T(8,128)(2,1)}, u32[]{:S(2)}, u32[]{:S(2)}) collective-permute-start(bf16[16,64,512]{2,1,0:T(8,128)(2,1)S(1)} %all-to-all-done.refs_0_), channel_id=1, source_target_pairs={{0,96},{32,0},{64,32},{96,64},{1,97},{33,1},{65,33},{97,65},{2,98}... | collective-permute-start | bytes 3145736 | tf_op jit(solution)/shard_map/ppermute | solution.py:20
  90.8 31.9 %collective-permute-start = (bf16[16,64,512]{2,1,0:T(8,128)(2,1)S(1)}, bf16[16,64,512]{2,1,0:T(8,128)(2,1)S(1)}, u32[]{:S(2)}, u32[]{:S(2)}) collective-permute-start(bf16[16,64,512]{2,1,0:T(8,128)(2,1)S(1)} %all-to-all-done.refs_0_), channel_id=1, source_target_pairs={{0,16},{16,0},{1,17},{17,1},{2,18},{18,2},{3,19},{19,3},{4,20},{20... | collective-permute-start | bytes 3145736 | tf_op jit(solution)/shard_map/ppermute | solution.py:24
  120.8 46.7 %collective-permute-start.28 = (bf16[768,512]{1,0:T(8,128)(2,1)}, bf16[768,512]{1,0:T(8,128)(2,1)}, u32[]{:S(2)}, u32[]{:S(2)}) collective-permute-start(bf16[768,512]{1,0:T(8,128)(2,1)} %collective-permute-done.27.refs_3_), channel_id=1, source_target_pairs={{0,3},{1,0},{2,1},{3,2},{4,7},{5,4},{6,5},{7,6},{8,11},{9,8},{10,9... | collective-permute-start | bytes 2359304 | tf_op jit(solution)/shard_map/ppermute | solution.py:20
  120.8 49.4 %collective-permute-start.31 = (bf16[768,512]{1,0:T(8,128)(2,1)}, bf16[768,512]{1,0:T(8,128)(2,1)}, u32[]{:S(2)}, u32[]{:S(2)}) collective-permute-start(bf16[768,512]{1,0:T(8,128)(2,1)} %collective-permute-done.30.refs_2_), channel_id=1, source_target_pairs={{0,1},{1,2},{2,3},{3,0},{4,5},{5,6},{6,7},{7,4},{8,9},{9,10},{10,1... | collective-permute-start | bytes 2359304 | tf_op jit(solution)/shard_map/ppermute | solution.py:20
  123.8 46.4 %collective-permute-start.32 = (bf16[768,512]{1,0:T(8,128)(2,1)}, bf16[768,512]{1,0:T(8,128)(2,1)S(1)}, u32[]{:S(2)}, u32[]{:S(2)}) collective-permute-start(bf16[768,512]{1,0:T(8,128)(2,1)} %collective-permute-done.27.refs_3_), channel_id=1, source_target_pairs={{0,1},{1,2},{2,3},{3,0},{4,5},{5,6},{6,7},{7,4},{8,9},{9,10},{10,1... | collective-permute-start | bytes 2359304 | tf_op jit(solution)/shard_map/ppermute | solution.py:20
  125.8 39.6 %collective-permute-start.17 = (bf16[384,512]{1,0:T(8,128)(2,1)S(1)}, bf16[384,512]{1,0:T(8,128)(2,1)}, u32[]{:S(2)}, u32[]{:S(2)}) collective-permute-start(bf16[384,512]{1,0:T(8,128)(2,1)S(1)} %slice.66), channel_id=1, source_target_pairs={{0,1},{1,2},{2,3},{3,0},{4,5},{5,6},{6,7},{7,4},{8,9},{9,10},{10,1... | collective-permute-start | bytes 1179656 | tf_op jit(solution)/shard_map/ppermute | solution.py:20
  126.4 39.0 %collective-permute-start.18 = (bf16[384,512]{1,0:T(8,128)(2,1)S(1)}, bf16[384,512]{1,0:T(8,128)(2,1)S(1)}, u32[]{:S(2)}, u32[]{:S(2)}) collective-permute-start(bf16[384,512]{1,0:T(8,128)(2,1)S(1)} %slice.67), channel_id=1, source_target_pairs={{0,3},{1,0},{2,1},{3,2},{4,7},{5,4},{6,5},{7,6},{8,11},{9,8},{10,9... | collective-permute-start | bytes 1179656 | tf_op jit(solution)/shard_map/ppermute | solution.py:20
  170.2 21.9 %collective-permute-start.15 = (bf16[768,512]{1,0:T(8,128)(2,1)}, bf16[768,512]{1,0:T(8,128)(2,1)}, u32[]{:S(2)}, u32[]{:S(2)}) collective-permute-start(bf16[768,512]{1,0:T(8,128)(2,1)} %collective-permute-done.14.refs_2_), channel_id=1, source_target_pairs={{0,4},{4,8},{8,12},{12,0},{1,5},{5,9},{9,13},{13,1},{2,6},{6,10},{... | collective-permute-start | bytes 2359304 | tf_op jit(solution)/shard_map/ppermute | solution.py:20
  171.1 33.5 %collective-permute-start.16 = (bf16[768,512]{1,0:T(8,128)(2,1)}, bf16[768,512]{1,0:T(8,128)(2,1)S(1)}, u32[]{:S(2)}, u32[]{:S(2)}) collective-permute-start(bf16[768,512]{1,0:T(8,128)(2,1)} %collective-permute-done.11.refs_3_), channel_id=1, source_target_pairs={{0,4},{4,8},{8,12},{12,0},{1,5},{5,9},{9,13},{13,1},{2,6},{6,10},{... | collective-permute-start | bytes 2359304 | tf_op jit(solution)/shard_map/ppermute | solution.py:20
  183.5 41.4 %collective-permute-start.2 = (bf16[16,64,512]{2,1,0:T(8,128)(2,1)}, bf16[16,64,512]{2,1,0:T(8,128)(2,1)}, u32[]{:S(2)}, u32[]{:S(2)}) collective-permute-start(bf16[16,64,512]{2,1,0:T(8,128)(2,1)} %collective-permute-done.1.refs_2_), channel_id=1, source_target_pairs={{0,16},{16,0},{1,17},{17,1},{2,18},{18,2},{3,19},{19,3},{4,20},{20... | collective-permute-start | bytes 3145736 | tf_op jit(solution)/shard_map/ppermute | solution.py:24
  184.8 40.1 %collective-permute-start.4 = (bf16[16,64,512]{2,1,0:T(8,128)(2,1)}, bf16[16,64,512]{2,1,0:T(8,128)(2,1)}, u32[]{:S(2)}, u32[]{:S(2)}) collective-permute-start(bf16[16,64,512]{2,1,0:T(8,128)(2,1)} %collective-permute-done.3.refs_4_), channel_id=1, source_target_pairs={{0,16},{16,0},{1,17},{17,1},{2,18},{18,2},{3,19},{19,3},{4,20},{20... | collective-permute-start | bytes 3145736 | tf_op jit(solution)/shard_map/ppermute | solution.py:24
  185.0 43.3 %collective-permute-start.6 = (bf16[16,64,512]{2,1,0:T(8,128)(2,1)}, bf16[16,64,512]{2,1,0:T(8,128)(2,1)}, u32[]{:S(2)}, u32[]{:S(2)}) collective-permute-start(bf16[16,64,512]{2,1,0:T(8,128)(2,1)} %collective-permute-done.5.refs_6_), channel_id=1, source_target_pairs={{0,16},{16,0},{1,17},{17,1},{2,18},{18,2},{3,19},{19,3},{4,20},{20... | collective-permute-start | bytes 3145736 | tf_op jit(solution)/shard_map/ppermute | solution.py:24
  207.1 30.2 %collective-permute-start.35 = (bf16[768,512]{1,0:T(8,128)(2,1)S(1)}, bf16[768,512]{1,0:T(8,128)(2,1)S(1)}, u32[]{:S(2)}, u32[]{:S(2)}) collective-permute-start(bf16[768,512]{1,0:T(8,128)(2,1)S(1)} %constant_dynamic-update-slice_fusion.2.refs_4_), channel_id=1, source_target_pairs={{0,1},{1,2},{2,3},{3,0},{4,5},{5,6},{6,7},{7,4},{8,9},{9,10},{10,1... | collective-permute-start | bytes 2359304 | tf_op jit(solution)/shard_map/ppermute | solution.py:20
  228.2 31.6 %collective-permute-start.29 = (bf16[768,512]{1,0:T(8,128)(2,1)}, bf16[768,512]{1,0:T(8,128)(2,1)S(1)}, u32[]{:S(2)}, u32[]{:S(2)}) collective-permute-start(bf16[768,512]{1,0:T(8,128)(2,1)} %collective-permute-done.28.refs_7_), channel_id=1, source_target_pairs={{0,3},{1,0},{2,1},{3,2},{4,7},{5,4},{6,5},{7,6},{8,11},{9,8},{10,9... | collective-permute-start | bytes 2359304 | tf_op jit(solution)/shard_map/ppermute | solution.py:20
  237.3 43.0 %collective-permute-start.41 = (bf16[768,512]{1,0:T(8,128)(2,1)}, bf16[768,512]{1,0:T(8,128)(2,1)S(1)}, u32[]{:S(2)}, u32[]{:S(2)}) collective-permute-start(bf16[768,512]{1,0:T(8,128)(2,1)} %collective-permute-done.31.refs_2_), channel_id=1, source_target_pairs={{0,1},{1,2},{2,3},{3,0},{4,5},{5,6},{6,7},{7,4},{8,9},{9,10},{10,1... | collective-permute-start | bytes 2359304 | tf_op jit(solution)/shard_map/ppermute | solution.py:20
  242.9 34.7 %collective-permute-start.13 = (bf16[768,512]{1,0:T(8,128)(2,1)}, bf16[768,512]{1,0:T(8,128)(2,1)S(1)}, u32[]{:S(2)}, u32[]{:S(2)}) collective-permute-start(bf16[768,512]{1,0:T(8,128)(2,1)} %collective-permute-done.12.refs_7_), channel_id=1, source_target_pairs={{0,12},{4,0},{8,4},{12,8},{1,13},{5,1},{9,5},{13,9},{2,14},{6,2},{... | collective-permute-start | bytes 2359304 | tf_op jit(solution)/shard_map/ppermute | solution.py:20
  242.9 37.4 %collective-permute-start.39 = (bf16[768,512]{1,0:T(8,128)(2,1)}, bf16[768,512]{1,0:T(8,128)(2,1)S(1)}, u32[]{:S(2)}, u32[]{:S(2)}) collective-permute-start(bf16[768,512]{1,0:T(8,128)(2,1)} %collective-permute-done.15.refs_2_), channel_id=1, source_target_pairs={{0,4},{4,8},{8,12},{12,0},{1,5},{5,9},{9,13},{13,1},{2,6},{6,10},{... | collective-permute-start | bytes 2359304 | tf_op jit(solution)/shard_map/ppermute | solution.py:20
  245.1 35.3 %collective-permute-start.42 = (bf16[768,512]{1,0:T(8,128)(2,1)S(1)}, bf16[768,512]{1,0:T(8,128)(2,1)S(1)}, u32[]{:S(2)}, u32[]{:S(2)}) collective-permute-start(bf16[768,512]{1,0:T(8,128)(2,1)S(1)} %collective-permute-done.38.refs_8_), channel_id=1, source_target_pairs={{0,3},{1,0},{2,1},{3,2},{4,7},{5,4},{6,5},{7,6},{8,11},{9,8},{10,9... | collective-permute-start | bytes 2359304 | tf_op jit(solution)/shard_map/ppermute | solution.py:20
  290.9 22.9 %collective-permute-start.43 = (bf16[4,192,512]{2,1,0:T(8,128)(2,1)}, bf16[4,192,512]{2,1,0:T(8,128)(2,1)}, u32[]{:S(2)}, u32[]{:S(2)}) collective-permute-start(bf16[4,192,512]{2,1,0:T(8,128)(2,1)} %get-tuple-element.10), channel_id=1, source_target_pairs={{0,16},{16,0},{1,17},{17,1},{2,18},{18,2},{3,19},{19,3},{4,20},{20... | collective-permute-start | bytes 2359304 | tf_op jit(solution)/shard_map/ppermute | solution.py:24
  297.7 23.8 %collective-permute-start.47 = (bf16[4,320,128]{2,1,0:T(8,128)(2,1)S(1)}, bf16[4,320,128]{2,1,0:T(8,128)(2,1)S(1)}, u32[]{:S(2)}, u32[]{:S(2)}) collective-permute-start(bf16[4,320,128]{2,1,0:T(8,128)(2,1)S(1)} %get-tuple-element.25), channel_id=1, source_target_pairs={{0,4},{4,8},{8,12},{12,0},{1,5},{5,9},{9,13},{13,1},{2,6},{6,10},{... | collective-permute-start | bytes 983048 | tf_op jit(solution)/shard_map/ppermute | solution.py:20
  315.2 22.8 %collective-permute-start.46 = (bf16[2,192,512]{2,1,0:T(8,128)(2,1)S(1)}, bf16[2,192,512]{2,1,0:T(8,128)(2,1)S(1)}, u32[]{:S(2)}, u32[]{:S(2)}) collective-permute-start(bf16[2,192,512]{2,1,0:T(8,128)(2,1)S(1)} %pad_maximum_fusion.10), channel_id=1, source_target_pairs={{0,96},{32,0},{64,32},{96,64},{1,97},{33,1},{65,33},{97,65},{2,98}... | collective-permute-start | bytes 1179656 | tf_op jit(solution)/shard_map/ppermute | solution.py:20
  (50 other events, 642.0 us)
where the time goes:
time: 371 us; the launch traced here: 370 us
  waiting for transfers between devices  197 us (53%)
  starting transfers between devices  96.4 us (26%)
  Pallas kernels  42.4 us (11%)
  local copies, waits for them, and re-layouts  28.9 us (8%)
    ppermute x53, waiting for transfers between devices, shift(): return lax.ppermute(x, axis, [(i, (i + step) % RING) for i in range(RING)])  193 us
    ppermute x53, starting transfers between devices, shift(): return lax.ppermute(x, axis, [(i, (i + step) % RING) for i in range(RING)])  81 us
    pallas_call x6, Pallas kernels, matmul(): pl.pallas_call(lambda *refs: matmul_body(len(parts), base is not None, *r...  25.2 us
    unnamed x44, local copies, waits for them, and re-layouts  9.51 us
    all_to_all x1, starting transfers between devices, loss_terms(): rows = lax.all_to_all(rows, AXES, split_axis=0, concat_axis=0, tiled=True)  9.02 us
    pallas_call x1, Pallas kernels, finish(): pl.pallas_call(lambda *refs: finish_body(len(LAST), local_rows, *refs), i...  7.55 us
  transfers between devices with their start and end apart: 61, of which 24 were waited for; matrix products, arithmetic and copies ran while one was open for 6% of the time, Pallas kernels for 9%

commit v1 on v0

--- a/solution.py
+++ b/solution.py
@@ -45,7 +45,7 @@
         in_specs=[pl.BlockSpec(memory_space=pltpu.SMEM)] + [vmem] * len(parts),
         out_specs=vmem,
         out_shape=jax.ShapeDtypeStruct((count, rows * len(parts), width), parts[0].dtype),
-        compiler_params=pltpu.CompilerParams(vmem_limit_bytes=24 << 20),
+        compiler_params=pltpu.CompilerParams(vmem_limit_bytes=20 << 20),
         name="assemble",
     )(places, *parts)
 
@@ -74,8 +74,10 @@
     half = own.shape[0] // 2
     left = shift(own, axis, 1)
     right = shift(own, axis, -1)
-    low = shift(left[:half], axis, 1)
-    high = shift(right[half:], axis, -1)
+    low = left[:half]
+    high = right[half:]
+    low = shift(low, axis, 1)
+    high = shift(high, axis, -1)
     return left, right, jnp.concatenate([low, high])
 
 
@@ -146,7 +148,7 @@
             transcendentals=0,
             bytes_accessed=2 * count * depth * (rows + width) + 4 * rows * width,
         ),
-        compiler_params=pltpu.CompilerParams(vmem_limit_bytes=24 << 20),
+        compiler_params=pltpu.CompilerParams(vmem_limit_bytes=20 << 20),
         name="embed",
     )(table, *operands)
 
@@ -261,7 +263,7 @@
         cost_estimate=pl.CostEstimate(
             flops=2 * count * count * width, transcendentals=0, bytes_accessed=8 * count * width
         ),
-        compiler_params=pltpu.CompilerParams(vmem_limit_bytes=40 << 20),
+        compiler_params=pltpu.CompilerParams(vmem_limit_bytes=20 << 20),
         name="finish",
     )(*tables, places, *operands)
 
@@ -378,10 +380,28 @@
     return value
 
 
+def pack_body(keep, swapped, *outs):
+    for n, out in enumerate(outs):
+        out[0] = keep[n]
+        out[1] = swapped[n]
+
+
+def pack(keep, swapped):
+    count, rows, width = keep.shape
+    vmem = pl.BlockSpec(memory_space=pltpu.VMEM)
+    return pl.pallas_call(
+        pack_body,
+        in_specs=[vmem] * 2,
+        out_specs=[vmem] * count,
+        out_shape=[jax.ShapeDtypeStruct((2, rows, width), keep.dtype)] * count,
+        compiler_params=pltpu.CompilerParams(vmem_limit_bytes=8 << 20),
+        name="pack",
+    )(keep, swapped)
+
+
 def exchange(keep, send):
-    swapped = swap(send)
-    pairs = [jnp.stack([keep[dz], swapped[dz]]) for dz in range(RING)]
-    return [pairs[dz] if dz == 0 else shift(pairs[dz], "dp_0", dz) for dz in range(RING)]
+    pairs = pack(keep, swap(send))
+    return [pairs[0]] + [shift(pairs[dz], "dp_0", dz) for dz in (1, 2, 3)]
 
 
 def local(crop_hidden, projector_weight, pairing):
@@ -413,15 +433,6 @@
     bases = [embed(pieces, weight, x_first) for pieces, x_first in zip(tops, (True, False))]
     sources = [(dz, dc) for dz in (0, 1, 3, 2) for dc in range(2)]
     places = jnp.stack([(plane - dz) % RING * 2 + (core ^ dc) for dz, dc in sources])
-    owned, keep, send, by_y, by_x, variance = finish(tops, weight, bases, places.astype(jnp.int32))
-    by_y = add(scatter(by_y, "mp_0")).astype(jnp.bfloat16)
-    by_x = add(scatter(by_x, "mp_1")).astype(jnp.bfloat16)
-    by_y = scatter(by_y, "mp_1")
-    by_x = scatter(by_x, "mp_0")
-
-    owned = owned.reshape(batch_rows, feature_part).T[:, None, :]
-
-    back = exchange(keep, send)
     turned = jnp.concatenate(
         [
             lax.dynamic_index_in_dim(pairing, crop_of(-dz, dc), 0, keepdims=True)
@@ -431,9 +442,23 @@
         axis=0,
     )
     anchors = jnp.stack([plane * 2 + (core ^ anchor) for anchor in range(2)]).astype(jnp.int32)
+    place = jnp.stack([lax.axis_index(MP), jnp.int32(batch_rows)]).astype(jnp.int32)
+    places, turned, anchors, place = lax.optimization_barrier(
+        (places.astype(jnp.int32), turned, anchors, place)
+    )
+    owned, keep, send, by_y, by_x, variance = finish(tops, weight, bases, places)
+    by_y = scatter(by_y, "mp_0")
+    by_x = scatter(by_x, "mp_1")
+    by_y = add(by_y).astype(jnp.bfloat16)
+    by_x = add(by_x).astype(jnp.bfloat16)
+    by_y = scatter(by_y, "mp_1")
+    by_x = scatter(by_x, "mp_0")
+
+    owned = owned.reshape(batch_rows, feature_part).T[:, None, :]
+
+    back = exchange(keep, send)
     invariance = distances(anchors, turned, back)
 
-    place = jnp.stack([lax.axis_index(MP), jnp.int32(batch_rows)]).astype(jnp.int32)
     rows = score(place, invariance, variance, by_y, by_x)
     scales = (
         1.0 / (2 * (crop_count - 1) * batch_rows * features),

time: 371 us -> 365 us (0.984)
  waiting for transfers between devices: 197 us -> 188 us
  local copies, waits for them, and re-layouts: 28.9 us -> 35 us
    ppermute x53, waiting for transfers between devices: 193 us -> 184 us  [shift(): return lax.ppermute(x, axis, [(i, (i + step) % RING) for i in range(RING)])]
    unnamed x44 -> x62, local copies, waits for them, and re-layouts: 9.51 us -> 13.1 us
  transfers between devices with their start and end apart: 61 -> 61, of which waited for: 24 -> 23; matrix products, arithmetic and copies ran while one was open for 6% -> 8% of each run, Pallas kernels for 9% -> 9%
where the time goes in v1:
time: 365 us; the launch traced here: 364 us
  waiting for transfers between devices  188 us (52%)
  starting transfers between devices  93.8 us (26%)
  Pallas kernels  41 us (11%)
  local copies, waits for them, and re-layouts  35 us (10%)
  other arithmetic  5.37 us (1%)
    ppermute x53, waiting for transfers between devices, shift(): return lax.ppermute(x, axis, [(i, (i + step) % RING) for i in range(RING)])  184 us
    ppermute x53, starting transfers between devices, shift(): return lax.ppermute(x, axis, [(i, (i + step) % RING) for i in range(RING)])  82 us
    pallas_call x6, Pallas kernels, matmul(): pl.pallas_call(lambda *refs: matmul_body(len(parts), base is not None, *r...  25.2 us
    unnamed x62, local copies, waits for them, and re-layouts  13.1 us
  transfers between devices with their start and end apart: 61, of which 23 were waited for; matrix products, arithmetic and copies ran while one was open for 8% of the time, Pallas kernels for 9%

profile of v1, /device:TPU:0, one launch (start us, length us, event | category | flops | bytes accessed | tf_op | source)
XLA Modules:
  0.0 364.2 jit_solution(4076203861916679555)
XLA Ops:
  4.9 4.2 %collective-permute-start.23 = (bf16[2,192,512]{2,1,0:T(8,128)(2,1)S(1)}, bf16[2,192,512]{2,1,0:T(8,128)(2,1)S(1)}, u32[]{:S(2)}, u32[]{:S(2)}) collective-permute-start(bf16[2,192,512]{2,1,0:T(8,128)(2,1)S(1)} %get-tuple-element.23), channel_id=1, source_target_pairs={{0,96},{32,0},{64,32},{96,64},{1,97},{33,1},{65,33},{97,65},{2,98}... | collective-permute-start | bytes 1179656 | tf_op jit(solution)/shard_map/ppermute | solution.py:20
  10.4 15.8 %collective-permute-done.23 = bf16[2,192,512]{2,1,0:T(8,128)(2,1)S(1)} collective-permute-done((bf16[2,192,512]{2,1,0:T(8,128)(2,1)S(1)}, bf16[2,192,512]{2,1,0:T(8,128)(2,1)S(1)}, u32[]{:S(2)}, u32[]{:S(2)}) %collective-permute-start.23) | collective-permute-done | bytes 393248 | tf_op jit(solution)/shard_map/ppermute | solution.py:20
  33.7 5.8 %all-to-all-start = ((bf16[16,64,512]{2,1,0:T(8,128)(2,1)}), bf16[16,64,512]{2,1,0:T(8,128)(2,1)S(1)}, u32[]{:S(2)}, u32[]{:S(2)}) async-start(bf16[16,64,512]{2,1,0:T(8,128)(2,1)} %bitcast.87), calls=%async_computation | async-start | bytes 2097152 | tf_op jit(solution)/shard_map/all_to_all | solution.py:59
  45.4 11.2 %collective-permute-done.30.refs_2_ = bf16[768,512]{1,0:T(8,128)(2,1)} collective-permute-done((bf16[768,512]{1,0:T(8,128)(2,1)S(1)}, bf16[768,512]{1,0:T(8,128)(2,1)}, u32[]{:S(2)}, u32[]{:S(2)}) %collective-permute-start.30) | collective-permute-done | bytes 786464 | tf_op jit(solution)/shard_map/ppermute | solution.py:20
  56.6 3.5 collective-permute-start.11
  62.5 8.0 %collective-permute-done.25.refs_1_ = bf16[768,512]{1,0:T(8,128)(2,1)} collective-permute-done((bf16[768,512]{1,0:T(8,128)(2,1)S(1)}, bf16[768,512]{1,0:T(8,128)(2,1)}, u32[]{:S(2)}, u32[]{:S(2)}) %collective-permute-start.25) | collective-permute-done | bytes 786464 | tf_op jit(solution)/shard_map/ppermute | solution.py:20
  72.2 3.4 collective-permute-start.3
  75.6 11.2 %collective-permute-done.14.refs_2_ = bf16[768,512]{1,0:T(8,128)(2,1)S(1)} collective-permute-done((bf16[768,512]{1,0:T(8,128)(2,1)S(1)}, bf16[768,512]{1,0:T(8,128)(2,1)S(1)}, u32[]{:S(2)}, u32[]{:S(2)}) %collective-permute-start.14) | collective-permute-done | bytes 786464 | tf_op jit(solution)/shard_map/ppermute | solution.py:20
  86.8 3.7 %collective-permute-start.5 = (bf16[16,64,512]{2,1,0:T(8,128)(2,1)S(1)}, bf16[16,64,512]{2,1,0:T(8,128)(2,1)}, u32[]{:S(2)}, u32[]{:S(2)}) collective-permute-start(bf16[16,64,512]{2,1,0:T(8,128)(2,1)S(1)} %all-to-all-done.refs_0_), channel_id=1, source_target_pairs={{0,96},{32,0},{64,32},{96,64},{1,97},{33,1},{65,33},{97,65},{2,98}... | collective-permute-start | bytes 3145736 | tf_op jit(solution)/shard_map/ppermute | solution.py:20
  94.1 17.7 %collective-permute-done.9.refs_1_ = bf16[768,512]{1,0:T(8,128)(2,1)} collective-permute-done((bf16[768,512]{1,0:T(8,128)(2,1)S(1)}, bf16[768,512]{1,0:T(8,128)(2,1)}, u32[]{:S(2)}, u32[]{:S(2)}) %collective-permute-start.9) | collective-permute-done | bytes 786464 | tf_op jit(solution)/shard_map/ppermute | solution.py:20
  115.0 5.5 %collective-permute-done.3.refs_4_ = bf16[16,64,512]{2,1,0:T(8,128)(2,1)} collective-permute-done((bf16[16,64,512]{2,1,0:T(8,128)(2,1)S(1)}, bf16[16,64,512]{2,1,0:T(8,128)(2,1)}, u32[]{:S(2)}, u32[]{:S(2)}) %collective-permute-start.3) | collective-permute-done | bytes 1048608 | tf_op jit(solution)/shard_map/ppermute | solution.py:20
  124.2 3.1 collective-permute-start.18
  127.3 37.8 %collective-permute-done.17 = bf16[384,512]{1,0:T(8,128)(2,1)S(1)} collective-permute-done((bf16[384,512]{1,0:T(8,128)(2,1)S(1)}, bf16[384,512]{1,0:T(8,128)(2,1)S(1)}, u32[]{:S(2)}, u32[]{:S(2)}) %collective-permute-start.17) | collective-permute-done | bytes 393248 | tf_op jit(solution)/shard_map/ppermute | solution.py:20
  171.6 10.7 %collective-permute-done.37.refs_6_ = bf16[768,512]{1,0:T(8,128)(2,1)S(1)} collective-permute-done((bf16[768,512]{1,0:T(8,128)(2,1)}, bf16[768,512]{1,0:T(8,128)(2,1)S(1)}, u32[]{:S(2)}, u32[]{:S(2)}) %collective-permute-start.37) | collective-permute-done | bytes 786464 | tf_op jit(solution)/shard_map/ppermute | solution.py:20
  185.1 6.5 %collective-permute-done.15.refs_2_ = bf16[768,512]{1,0:T(8,128)(2,1)S(1)} collective-permute-done((bf16[768,512]{1,0:T(8,128)(2,1)S(1)}, bf16[768,512]{1,0:T(8,128)(2,1)S(1)}, u32[]{:S(2)}, u32[]{:S(2)}) %collective-permute-start.15) | collective-permute-done | bytes 786464 | tf_op jit(solution)/shard_map/ppermute | solution.py:20
  191.5 12.6 %collective-permute-done.16.refs_3_ = bf16[768,512]{1,0:T(8,128)(2,1)S(1)} collective-permute-done((bf16[768,512]{1,0:T(8,128)(2,1)}, bf16[768,512]{1,0:T(8,128)(2,1)S(1)}, u32[]{:S(2)}, u32[]{:S(2)}) %collective-permute-start.16) | collective-permute-done | bytes 786464 | tf_op jit(solution)/shard_map/ppermute | solution.py:20
  211.3 10.6 %collective-permute-done.10.refs_1_ = bf16[768,512]{1,0:T(8,128)(2,1)} collective-permute-done((bf16[768,512]{1,0:T(8,128)(2,1)}, bf16[768,512]{1,0:T(8,128)(2,1)}, u32[]{:S(2)}, u32[]{:S(2)}) %collective-permute-start.10) | collective-permute-done | bytes 786464 | tf_op jit(solution)/shard_map/ppermute | solution.py:20
  224.3 3.2 collective-permute-start.22
  229.6 3.7 %assemble.1.refs_5_.refs_9_.refs_3_ = bf16[16,512,512]{2,1,0:T(8,128)(2,1)S(1)} custom-call(s32[8]{0:T(128)S(1)} %stack.186.places, bf16[16,64,512]{2,1,0:T(8,128)(2,1)S(1)} %all-to-all-done.refs_0_, bf16[16,64,512]{2,1,0:T(8,128)(2,1)S(1)} %copy-done.3, bf16[16,64,512]{2,1,0:T(8,128)(2,1)} %collective-permute-done.1.refs_2_, ...), custom_call_target="tpu_custom_call" | custom-call | tf_op jit(solution)/shard_map/assemble/pallas_call | solution.py:43
  233.4 4.1 %embed.9.refs_10_ = f32[768,512]{1,0:T(8,128)S(1)} custom-call(s32[4]{0:T(128)S(1)} %pad_add_fusion.7.refs_0_, bf16[768,512]{1,0:T(8,128)(2,1)S(1)} %pad_maximum_fusion.3.refs_1_, bf16[768,512]{1,0:T(8,128)(2,1)} %collective-permute-done.30.refs_2_, bf16[768,512]{1,0:T(8,128)(2,1)} %collective-permute-done.27.refs_3_, ...), custom_call_target="tpu_custom_call" | custom-call | flops 1610612736 | bytes 6815744 | tf_op jit(solution)/shard_map/embed/pallas_call | solution.py:141
  244.7 3.6 collective-permute-start.42
  248.3 11.2 %collective-permute-done.29.refs_2_ = bf16[768,512]{1,0:T(8,128)(2,1)} collective-permute-done((bf16[768,512]{1,0:T(8,128)(2,1)}, bf16[768,512]{1,0:T(8,128)(2,1)}, u32[]{:S(2)}, u32[]{:S(2)}) %collective-permute-start.29) | collective-permute-done | bytes 786464 | tf_op jit(solution)/shard_map/ppermute | solution.py:20
  259.5 3.7 %embed.6.refs_10_ = f32[768,512]{1,0:T(8,128)S(1)} custom-call(s32[4]{0:T(128)S(1)} %pad_add_fusion.5.refs_0_, bf16[768,512]{1,0:T(8,128)(2,1)S(1)} %pad_maximum_fusion.2.refs_1_, bf16[768,512]{1,0:T(8,128)(2,1)S(1)} %collective-permute-done.14.refs_2_, bf16[768,512]{1,0:T(8,128)(2,1)} %collective-permute-done.11.refs_3_, ...), custom_call_target="tpu_custom_call" | custom-call | flops 1610612736 | bytes 6815744 | tf_op jit(solution)/shard_map/embed/pallas_call | solution.py:141
  263.2 6.1 %embed.10.refs_4_ = f32[768,512]{1,0:T(8,128)S(1)} custom-call(s32[8]{0:T(128)S(1)} %stack.206.refs_0_, bf16[768,512]{1,0:T(8,128)(2,1)} %collective-permute-done.25.refs_1_, bf16[768,512]{1,0:T(8,128)(2,1)S(1)} %copy-done.5, bf16[768,512]{1,0:T(8,128)(2,1)S(1)} %copy-done.7, bf16[768,512]{1,0:T(8,128)(2,1)} %collective-permute-done.35.refs_4_, ...), custom_call_target="tpu_custom_call" | custom-call | flops 3221225472 | bytes 12058624 | tf_op jit(solution)/shard_map/embed/pallas_call | solution.py:141
  269.3 6.1 %embed.7.refs_4_ = f32[768,512]{1,0:T(8,128)S(1)} custom-call(s32[8]{0:T(128)S(1)} %stack.199.refs_0_, bf16[768,512]{1,0:T(8,128)(2,1)} %collective-permute-done.9.refs_1_, bf16[768,512]{1,0:T(8,128)(2,1)S(1)} %copy-done.9, bf16[768,512]{1,0:T(8,128)(2,1)S(1)} %copy-done.15, bf16[768,512]{1,0:T(8,128)(2,1)} %collective-permute-done.19.refs_4_, ...), custom_call_target="tpu_custom_call" | custom-call | flops 3221225472 | bytes 12058624 | tf_op jit(solution)/shard_map/embed/pallas_call | solution.py:141
  280.8 4.7 %finish.1 = (f32[8,192,512]{2,1,0:T(8,128)S(1)}, bf16[4,192,512]{2,1,0:T(8,128)(2,1)S(1)}, bf16[4,192,512]{2,1,0:T(8,128)(2,1)}, bf16[4,4,320,128]{3,2,1,0:T(8,1...) custom-call(s32[2]{0:T(128)S(1)} %get-tuple-element.68.refs_0_, ...), custom_call_target="tpu_custom_call" | custom-call | flops 2415919104 | bytes 6291456 | tf_op jit(solution)/shard_map/finish/pallas_call | solution.py:247
  303.1 6.3 %collective-permute-done.54 = bf16[4,320,128]{2,1,0:T(8,128)(2,1)} collective-permute-done((bf16[4,320,128]{2,1,0:T(8,128)(2,1)}, bf16[4,320,128]{2,1,0:T(8,128)(2,1)}, u32[]{:S(2)}, u32[]{:S(2)}) %collective-permute-start.54) | collective-permute-done | bytes 327712 | tf_op jit(solution)/shard_map/ppermute | solution.py:20
  314.0 4.4 %collective-permute-start.44 = (bf16[2,192,512]{2,1,0:T(8,128)(2,1)S(1)}, bf16[2,192,512]{2,1,0:T(8,128)(2,1)S(1)}, u32[]{:S(2)}, u32[]{:S(2)}) collective-permute-start(bf16[2,192,512]{2,1,0:T(8,128)(2,1)S(1)} %get-tuple-element.32), channel_id=1, source_target_pairs={{0,32},{32,64},{64,96},{96,0},{1,33},{33,65},{65,97},{97,1},{2,34}... | collective-permute-start | bytes 1179656 | tf_op jit(solution)/shard_map/ppermute | solution.py:20
  318.4 3.4 collective-permute-start.45
  330.6 8.3 %collective-permute-done.45.refs_2_ = bf16[2,192,512]{2,1,0:T(8,128)(2,1)S(1)} collective-permute-done((bf16[2,192,512]{2,1,0:T(8,128)(2,1)S(1)}, bf16[2,192,512]{2,1,0:T(8,128)(2,1)S(1)}, u32[]{:S(2)}, u32[]{:S(2)}) %collective-permute-start.45) | collective-permute-done | bytes 393248 | tf_op jit(solution)/shard_map/ppermute | solution.py:20
  347.9 5.4 %all-to-all-start.1 = ((f32[128,1,128]{2,1,0:T(1,128)}), f32[128,1,128]{2,1,0:T(1,128)S(1)}, u32[]{:S(2)}, u32[]{:S(2)}) async-start(f32[128,1,128]{2,1,0:T(1,128)} %bitcast.55), calls=%async_computation.1 | async-start | bytes 131072 | tf_op jit(solution)/shard_map/all_to_all | solution.py:328
  355.6 5.7 %broadcast_in_dim.3 = f32[512,1,1536]{2,1,0:T(1,128)} reshape(f32[512,1536]{1,0:T(8,128)} %bitcast.85) | data formatting | bytes 6291456 | tf_op jit(solution)/shard_map/broadcast_in_dim | solution.py:457
  (197 shorter events, 111.5 us)
Async XLA Ops:
  4.9 21.3 %collective-permute-start.23 = (bf16[2,192,512]{2,1,0:T(8,128)(2,1)S(1)}, bf16[2,192,512]{2,1,0:T(8,128)(2,1)S(1)}, u32[]{:S(2)}, u32[]{:S(2)}) collective-permute-start(bf16[2,192,512]{2,1,0:T(8,128)(2,1)S(1)} %get-tuple-element.23), channel_id=1, source_target_pairs={{0,96},{32,0},{64,32},{96,64},{1,97},{33,1},{65,33},{97,65},{2,98}... | collective-permute-start | bytes 1179656 | tf_op jit(solution)/shard_map/ppermute | solution.py:20
  9.1 33.7 %collective-permute-start.8 = (bf16[2,192,512]{2,1,0:T(8,128)(2,1)S(1)}, bf16[2,192,512]{2,1,0:T(8,128)(2,1)S(1)}, u32[]{:S(2)}, u32[]{:S(2)}) collective-permute-start(bf16[2,192,512]{2,1,0:T(8,128)(2,1)S(1)} %get-tuple-element.22), channel_id=1, source_target_pairs={{0,32},{32,64},{64,96},{96,0},{1,33},{33,65},{65,97},{97,1},{2,34}... | collective-permute-start | bytes 1179656 | tf_op jit(solution)/shard_map/ppermute | solution.py:20
  28.0 28.6 %collective-permute-start.30 = (bf16[768,512]{1,0:T(8,128)(2,1)S(1)}, bf16[768,512]{1,0:T(8,128)(2,1)}, u32[]{:S(2)}, u32[]{:S(2)}) collective-permute-start(bf16[768,512]{1,0:T(8,128)(2,1)S(1)} %pad_maximum_fusion.3.refs_1_), channel_id=1, source_target_pairs={{0,4},{4,8},{8,12},{12,0},{1,5},{5,9},{9,13},{13,1},{2,6},{6,10},{... | collective-permute-start | bytes 2359304 | tf_op jit(solution)/shard_map/ppermute | solution.py:20
  29.6 30.4 %collective-permute-start.27 = (bf16[768,512]{1,0:T(8,128)(2,1)S(1)}, bf16[768,512]{1,0:T(8,128)(2,1)}, u32[]{:S(2)}, u32[]{:S(2)}) collective-permute-start(bf16[768,512]{1,0:T(8,128)(2,1)S(1)} %pad_maximum_fusion.3.refs_1_), channel_id=1, source_target_pairs={{0,12},{4,0},{8,4},{12,8},{1,13},{5,1},{9,5},{13,9},{2,14},{6,2},{... | collective-permute-start | bytes 2359304 | tf_op jit(solution)/shard_map/ppermute | solution.py:20
  33.7 28.8 %all-to-all-start = ((bf16[16,64,512]{2,1,0:T(8,128)(2,1)}), bf16[16,64,512]{2,1,0:T(8,128)(2,1)S(1)}, u32[]{:S(2)}, u32[]{:S(2)}) async-start(bf16[16,64,512]{2,1,0:T(8,128)(2,1)} %bitcast.87), calls=%async_computation | async-start | bytes 2097152 | tf_op jit(solution)/shard_map/all_to_all | solution.py:59
  39.5 31.0 %collective-permute-start.25 = (bf16[768,512]{1,0:T(8,128)(2,1)S(1)}, bf16[768,512]{1,0:T(8,128)(2,1)}, u32[]{:S(2)}, u32[]{:S(2)}) collective-permute-start(bf16[768,512]{1,0:T(8,128)(2,1)S(1)} %pad_maximum_fusion.3.refs_1_), channel_id=1, source_target_pairs={{0,1},{1,2},{2,3},{3,0},{4,5},{5,6},{6,7},{7,4},{8,9},{9,10},{10,1... | collective-permute-start | bytes 2359304 | tf_op jit(solution)/shard_map/ppermute | solution.py:20
  41.4 30.8 %collective-permute-start.36 = (bf16[768,512]{1,0:T(8,128)(2,1)S(1)}, bf16[768,512]{1,0:T(8,128)(2,1)}, u32[]{:S(2)}, u32[]{:S(2)}) collective-permute-start(bf16[768,512]{1,0:T(8,128)(2,1)S(1)} %pad_maximum_fusion.3.refs_1_), channel_id=1, source_target_pairs={{0,3},{1,0},{2,1},{3,2},{4,7},{5,4},{6,5},{7,6},{8,11},{9,8},{10,9... | collective-permute-start | bytes 2359304 | tf_op jit(solution)/shard_map/ppermute | solution.py:20
  44.7 42.2 %collective-permute-start.14 = (bf16[768,512]{1,0:T(8,128)(2,1)S(1)}, bf16[768,512]{1,0:T(8,128)(2,1)S(1)}, u32[]{:S(2)}, u32[]{:S(2)}) collective-permute-start(bf16[768,512]{1,0:T(8,128)(2,1)S(1)} %pad_maximum_fusion.2.refs_1_), channel_id=1, source_target_pairs={{0,1},{1,2},{2,3},{3,0},{4,5},{5,6},{6,7},{7,4},{8,9},{9,10},{10,1... | collective-permute-start | bytes 2359304 | tf_op jit(solution)/shard_map/ppermute | solution.py:20
  56.6 33.9 %collective-permute-start.11 = (bf16[768,512]{1,0:T(8,128)(2,1)S(1)}, bf16[768,512]{1,0:T(8,128)(2,1)}, u32[]{:S(2)}, u32[]{:S(2)}) collective-permute-start(bf16[768,512]{1,0:T(8,128)(2,1)S(1)} %pad_maximum_fusion.2.refs_1_), channel_id=1, source_target_pairs={{0,3},{1,0},{2,1},{3,2},{4,7},{5,4},{6,5},{7,6},{8,11},{9,8},{10,9... | collective-permute-start | bytes 2359304 | tf_op jit(solution)/shard_map/ppermute | solution.py:20
  60.1 30.4 %collective-permute-start.20 = (bf16[768,512]{1,0:T(8,128)(2,1)S(1)}, bf16[768,512]{1,0:T(8,128)(2,1)}, u32[]{:S(2)}, u32[]{:S(2)}) collective-permute-start(bf16[768,512]{1,0:T(8,128)(2,1)S(1)} %pad_maximum_fusion.2.refs_1_), channel_id=1, source_target_pairs={{0,12},{4,0},{8,4},{12,8},{1,13},{5,1},{9,5},{13,9},{2,14},{6,2},{... | collective-permute-start | bytes 2359304 | tf_op jit(solution)/shard_map/ppermute | solution.py:20
  70.5 41.6 %collective-permute-start.1 = (bf16[16,64,512]{2,1,0:T(8,128)(2,1)S(1)}, bf16[16,64,512]{2,1,0:T(8,128)(2,1)}, u32[]{:S(2)}, u32[]{:S(2)}) collective-permute-start(bf16[16,64,512]{2,1,0:T(8,128)(2,1)S(1)} %all-to-all-done.refs_0_), channel_id=1, source_target_pairs={{0,32},{32,64},{64,96},{96,0},{1,33},{33,65},{65,97},{97,1},{2,34}... | collective-permute-start | bytes 3145736 | tf_op jit(solution)/shard_map/ppermute | solution.py:20
  72.2 48.3 %collective-permute-start.3 = (bf16[16,64,512]{2,1,0:T(8,128)(2,1)S(1)}, bf16[16,64,512]{2,1,0:T(8,128)(2,1)}, u32[]{:S(2)}, u32[]{:S(2)}) collective-permute-start(bf16[16,64,512]{2,1,0:T(8,128)(2,1)S(1)} %all-to-all-done.refs_0_), channel_id=1, source_target_pairs={{0,64},{32,96},{64,0},{96,32},{1,65},{33,97},{65,1},{97,33},{2,66}... | collective-permute-start | bytes 3145736 | tf_op jit(solution)/shard_map/ppermute | solution.py:20
  86.8 33.7 %collective-permute-start.5 = (bf16[16,64,512]{2,1,0:T(8,128)(2,1)S(1)}, bf16[16,64,512]{2,1,0:T(8,128)(2,1)}, u32[]{:S(2)}, u32[]{:S(2)}) collective-permute-start(bf16[16,64,512]{2,1,0:T(8,128)(2,1)S(1)} %all-to-all-done.refs_0_), channel_id=1, source_target_pairs={{0,96},{32,0},{64,32},{96,64},{1,97},{33,1},{65,33},{97,65},{2,98}... | collective-permute-start | bytes 3145736 | tf_op jit(solution)/shard_map/ppermute | solution.py:20
  90.5 32.1 %collective-permute-start = (bf16[16,64,512]{2,1,0:T(8,128)(2,1)S(1)}, bf16[16,64,512]{2,1,0:T(8,128)(2,1)S(1)}, u32[]{:S(2)}, u32[]{:S(2)}) collective-permute-start(bf16[16,64,512]{2,1,0:T(8,128)(2,1)S(1)} %all-to-all-done.refs_0_), channel_id=1, source_target_pairs={{0,16},{16,0},{1,17},{17,1},{2,18},{18,2},{3,19},{19,3},{4,20},{20... | collective-permute-start | bytes 3145736 | tf_op jit(solution)/shard_map/ppermute | solution.py:24
  120.5 46.6 %collective-permute-start.28 = (bf16[768,512]{1,0:T(8,128)(2,1)}, bf16[768,512]{1,0:T(8,128)(2,1)}, u32[]{:S(2)}, u32[]{:S(2)}) collective-permute-start(bf16[768,512]{1,0:T(8,128)(2,1)} %collective-permute-done.27.refs_3_), channel_id=1, source_target_pairs={{0,3},{1,0},{2,1},{3,2},{4,7},{5,4},{6,5},{7,6},{8,11},{9,8},{10,9... | collective-permute-start | bytes 2359304 | tf_op jit(solution)/shard_map/ppermute | solution.py:20
  120.5 49.4 %collective-permute-start.31 = (bf16[768,512]{1,0:T(8,128)(2,1)}, bf16[768,512]{1,0:T(8,128)(2,1)S(1)}, u32[]{:S(2)}, u32[]{:S(2)}) collective-permute-start(bf16[768,512]{1,0:T(8,128)(2,1)} %collective-permute-done.30.refs_2_), channel_id=1, source_target_pairs={{0,1},{1,2},{2,3},{3,0},{4,5},{5,6},{6,7},{7,4},{8,9},{9,10},{10,1... | collective-permute-start | bytes 2359304 | tf_op jit(solution)/shard_map/ppermute | solution.py:20
  122.6 47.3 %collective-permute-start.32 = (bf16[768,512]{1,0:T(8,128)(2,1)}, bf16[768,512]{1,0:T(8,128)(2,1)S(1)}, u32[]{:S(2)}, u32[]{:S(2)}) collective-permute-start(bf16[768,512]{1,0:T(8,128)(2,1)} %collective-permute-done.27.refs_3_), channel_id=1, source_target_pairs={{0,1},{1,2},{2,3},{3,0},{4,5},{5,6},{6,7},{7,4},{8,9},{9,10},{10,1... | collective-permute-start | bytes 2359304 | tf_op jit(solution)/shard_map/ppermute | solution.py:20
  124.0 41.1 %collective-permute-start.17 = (bf16[384,512]{1,0:T(8,128)(2,1)S(1)}, bf16[384,512]{1,0:T(8,128)(2,1)S(1)}, u32[]{:S(2)}, u32[]{:S(2)}) collective-permute-start(bf16[384,512]{1,0:T(8,128)(2,1)S(1)} %slice.16), channel_id=1, source_target_pairs={{0,1},{1,2},{2,3},{3,0},{4,5},{5,6},{6,7},{7,4},{8,9},{9,10},{10,1... | collective-permute-start | bytes 1179656 | tf_op jit(solution)/shard_map/ppermute | solution.py:20
  124.2 40.9 %collective-permute-start.18 = (bf16[384,512]{1,0:T(8,128)(2,1)S(1)}, bf16[384,512]{1,0:T(8,128)(2,1)S(1)}, u32[]{:S(2)}, u32[]{:S(2)}) collective-permute-start(bf16[384,512]{1,0:T(8,128)(2,1)S(1)} %slice.17), channel_id=1, source_target_pairs={{0,3},{1,0},{2,1},{3,2},{4,7},{5,4},{6,5},{7,6},{8,11},{9,8},{10,9... | collective-permute-start | bytes 1179656 | tf_op jit(solution)/shard_map/ppermute | solution.py:20
  169.9 21.6 %collective-permute-start.15 = (bf16[768,512]{1,0:T(8,128)(2,1)S(1)}, bf16[768,512]{1,0:T(8,128)(2,1)S(1)}, u32[]{:S(2)}, u32[]{:S(2)}) collective-permute-start(bf16[768,512]{1,0:T(8,128)(2,1)S(1)} %collective-permute-done.14.refs_2_), channel_id=1, source_target_pairs={{0,4},{4,8},{8,12},{12,0},{1,5},{5,9},{9,13},{13,1},{2,6},{6,10},{... | collective-permute-start | bytes 2359304 | tf_op jit(solution)/shard_map/ppermute | solution.py:20
  170.8 33.3 %collective-permute-start.16 = (bf16[768,512]{1,0:T(8,128)(2,1)}, bf16[768,512]{1,0:T(8,128)(2,1)S(1)}, u32[]{:S(2)}, u32[]{:S(2)}) collective-permute-start(bf16[768,512]{1,0:T(8,128)(2,1)} %collective-permute-done.11.refs_3_), channel_id=1, source_target_pairs={{0,4},{4,8},{8,12},{12,0},{1,5},{5,9},{9,13},{13,1},{2,6},{6,10},{... | collective-permute-start | bytes 2359304 | tf_op jit(solution)/shard_map/ppermute | solution.py:20
  183.2 41.1 %collective-permute-start.2 = (bf16[16,64,512]{2,1,0:T(8,128)(2,1)}, bf16[16,64,512]{2,1,0:T(8,128)(2,1)}, u32[]{:S(2)}, u32[]{:S(2)}) collective-permute-start(bf16[16,64,512]{2,1,0:T(8,128)(2,1)} %collective-permute-done.1.refs_2_), channel_id=1, source_target_pairs={{0,16},{16,0},{1,17},{17,1},{2,18},{18,2},{3,19},{19,3},{4,20},{20... | collective-permute-start | bytes 3145736 | tf_op jit(solution)/shard_map/ppermute | solution.py:24
  184.5 39.8 %collective-permute-start.4 = (bf16[16,64,512]{2,1,0:T(8,128)(2,1)}, bf16[16,64,512]{2,1,0:T(8,128)(2,1)}, u32[]{:S(2)}, u32[]{:S(2)}) collective-permute-start(bf16[16,64,512]{2,1,0:T(8,128)(2,1)} %collective-permute-done.3.refs_4_), channel_id=1, source_target_pairs={{0,16},{16,0},{1,17},{17,1},{2,18},{18,2},{3,19},{19,3},{4,20},{20... | collective-permute-start | bytes 3145736 | tf_op jit(solution)/shard_map/ppermute | solution.py:24
  184.6 42.9 %collective-permute-start.6 = (bf16[16,64,512]{2,1,0:T(8,128)(2,1)}, bf16[16,64,512]{2,1,0:T(8,128)(2,1)}, u32[]{:S(2)}, u32[]{:S(2)}) collective-permute-start(bf16[16,64,512]{2,1,0:T(8,128)(2,1)} %collective-permute-done.5.refs_6_), channel_id=1, source_target_pairs={{0,16},{16,0},{1,17},{17,1},{2,18},{18,2},{3,19},{19,3},{4,20},{20... | collective-permute-start | bytes 3145736 | tf_op jit(solution)/shard_map/ppermute | solution.py:24
  210.4 27.1 %collective-permute-start.35 = (bf16[768,512]{1,0:T(8,128)(2,1)}, bf16[768,512]{1,0:T(8,128)(2,1)}, u32[]{:S(2)}, u32[]{:S(2)}) collective-permute-start(bf16[768,512]{1,0:T(8,128)(2,1)} %constant_dynamic-update-slice_fusion.2.refs_4_), channel_id=1, source_target_pairs={{0,1},{1,2},{2,3},{3,0},{4,5},{5,6},{6,7},{7,4},{8,9},{9,10},{10,1... | collective-permute-start | bytes 2359304 | tf_op jit(solution)/shard_map/ppermute | solution.py:20
  227.6 31.9 %collective-permute-start.29 = (bf16[768,512]{1,0:T(8,128)(2,1)}, bf16[768,512]{1,0:T(8,128)(2,1)}, u32[]{:S(2)}, u32[]{:S(2)}) collective-permute-start(bf16[768,512]{1,0:T(8,128)(2,1)} %collective-permute-done.28.refs_7_), channel_id=1, source_target_pairs={{0,3},{1,0},{2,1},{3,2},{4,7},{5,4},{6,5},{7,6},{8,11},{9,8},{10,9... | collective-permute-start | bytes 2359304 | tf_op jit(solution)/shard_map/ppermute | solution.py:20
  237.5 43.3 %collective-permute-start.41 = (bf16[768,512]{1,0:T(8,128)(2,1)S(1)}, bf16[768,512]{1,0:T(8,128)(2,1)S(1)}, u32[]{:S(2)}, u32[]{:S(2)}) collective-permute-start(bf16[768,512]{1,0:T(8,128)(2,1)S(1)} %copy-done.5), channel_id=1, source_target_pairs={{0,1},{1,2},{2,3},{3,0},{4,5},{5,6},{6,7},{7,4},{8,9},{9,10},{10,1... | collective-permute-start | bytes 2359304 | tf_op jit(solution)/shard_map/ppermute | solution.py:20
  242.6 35.5 %collective-permute-start.13 = (bf16[768,512]{1,0:T(8,128)(2,1)S(1)}, bf16[768,512]{1,0:T(8,128)(2,1)S(1)}, u32[]{:S(2)}, u32[]{:S(2)}) collective-permute-start(bf16[768,512]{1,0:T(8,128)(2,1)S(1)} %copy-done.11), channel_id=1, source_target_pairs={{0,12},{4,0},{8,4},{12,8},{1,13},{5,1},{9,5},{13,9},{2,14},{6,2},{... | collective-permute-start | bytes 2359304 | tf_op jit(solution)/shard_map/ppermute | solution.py:20
  242.7 38.1 %collective-permute-start.39 = (bf16[768,512]{1,0:T(8,128)(2,1)S(1)}, bf16[768,512]{1,0:T(8,128)(2,1)S(1)}, u32[]{:S(2)}, u32[]{:S(2)}) collective-permute-start(bf16[768,512]{1,0:T(8,128)(2,1)S(1)} %copy-done.9), channel_id=1, source_target_pairs={{0,4},{4,8},{8,12},{12,0},{1,5},{5,9},{9,13},{13,1},{2,6},{6,10},{... | collective-permute-start | bytes 2359304 | tf_op jit(solution)/shard_map/ppermute | solution.py:20
  244.7 36.1 %collective-permute-start.42 = (bf16[768,512]{1,0:T(8,128)(2,1)}, bf16[768,512]{1,0:T(8,128)(2,1)S(1)}, u32[]{:S(2)}, u32[]{:S(2)}) collective-permute-start(bf16[768,512]{1,0:T(8,128)(2,1)} %collective-permute-done.38.refs_8_), channel_id=1, source_target_pairs={{0,3},{1,0},{2,1},{3,2},{4,7},{5,4},{6,5},{7,6},{8,11},{9,8},{10,9... | collective-permute-start | bytes 2359304 | tf_op jit(solution)/shard_map/ppermute | solution.py:20
  288.6 24.2 %collective-permute-start.43 = (bf16[4,192,512]{2,1,0:T(8,128)(2,1)}, bf16[4,192,512]{2,1,0:T(8,128)(2,1)}, u32[]{:S(2)}, u32[]{:S(2)}) collective-permute-start(bf16[4,192,512]{2,1,0:T(8,128)(2,1)} %get-tuple-element.30), channel_id=1, source_target_pairs={{0,16},{16,0},{1,17},{17,1},{2,18},{18,2},{3,19},{19,3},{4,20},{20... | collective-permute-start | bytes 2359304 | tf_op jit(solution)/shard_map/ppermute | solution.py:24
  298.1 23.8 %collective-permute-start.47 = (bf16[4,320,128]{2,1,0:T(8,128)(2,1)}, bf16[4,320,128]{2,1,0:T(8,128)(2,1)}, u32[]{:S(2)}, u32[]{:S(2)}) collective-permute-start(bf16[4,320,128]{2,1,0:T(8,128)(2,1)} %get-tuple-element.49), channel_id=1, source_target_pairs={{0,4},{4,8},{8,12},{12,0},{1,5},{5,9},{9,13},{13,1},{2,6},{6,10},{... | collective-permute-start | bytes 983048 | tf_op jit(solution)/shard_map/ppermute | solution.py:20
  (59 other events, 886.1 us)

commit v2 on v1

--- a/solution.py
+++ b/solution.py
@@ -84,14 +84,38 @@
 OWN, LEFT, RIGHT, FAR = 0, -1, 1, 2
 
 
+def split_gather(first, second, first_axis, second_axis):
+    parts = {}
+    for tag, x in (("0", first), ("1", second)):
+        parts[tag] = [
+            shift(x, first_axis, 1),
+            shift(x, first_axis, -1),
+            shift(x, second_axis, 1),
+            shift(x, second_axis, -1),
+        ]
+    low = shift(parts["0"][0], first_axis, 1)
+    high = shift(parts["1"][1], first_axis, -1)
+    left, right, above, below = (jnp.concatenate(pair) for pair in zip(*parts.values()))
+    own, far = jnp.concatenate([first, second]), jnp.concatenate([low, high])
+    return spread(own, left, right, far, second_axis, (above, below))
+
+
 def plane_gather(own, first_axis, second_axis):
     left, right, far = ring(own, first_axis)
+    return spread(own, left, right, far, second_axis)
+
+
+def spread(own, left, right, far, second_axis, moved=None):
     row = {OWN: own, LEFT: left, RIGHT: right, FAR: far}
     pieces = {(OWN, early): x for early, x in row.items()}
+    if moved:
+        pieces[LEFT, OWN], pieces[RIGHT, OWN] = moved
     for early in (OWN, LEFT, RIGHT, FAR):
-        pieces[LEFT, early] = shift(row[early], second_axis, 1)
+        if (LEFT, early) not in pieces:
+            pieces[LEFT, early] = shift(row[early], second_axis, 1)
     for early in (OWN, RIGHT, LEFT, FAR):
-        pieces[RIGHT, early] = shift(row[early], second_axis, -1)
+        if (RIGHT, early) not in pieces:
+            pieces[RIGHT, early] = shift(row[early], second_axis, -1)
     for late, early, step in ((LEFT, OWN, 1), (LEFT, LEFT, 1), (RIGHT, RIGHT, -1), (RIGHT, FAR, -1)):
         pieces[FAR, early] = shift(pieces[late, early], second_axis, step)
     return pieces
@@ -177,21 +201,27 @@
     count, width = values.shape
     mean = jnp.zeros((1, width), jnp.float32)
     for h in range(2):
-        products(parts[h], weight, tables[h], bases[h], values, h * (count // 2), True)
-    for start in range(0, count, local_rows):
-        value = values[start : start + local_rows, :]
-        mean = mean + jnp.sum(value, axis=0, keepdims=True)
-        at = start // local_rows
-        owned[places[at]] = value
-        back = (0, 3, 1, 2)[at // 2]
-        out = send if at % 2 else keep
-        out[back] = value.astype(out.dtype)
-    mean = mean / count
-    square = jnp.zeros_like(mean)
-    for start in range(0, count, local_rows):
-        centered = values[start : start + local_rows, :] - mean
-        square = square + jnp.sum(centered * centered, axis=0, keepdims=True)
-        rows[start : start + local_rows, :] = centered.astype(rows.dtype)
+        products(parts[h], weight, tables[h], bases[h], values, h * (count // 2))
+
+    def take(k, total):
+        back = lax.select(k == 0, 0, lax.select(k == 1, 3, k - 1))
+        for c, out in enumerate((keep, send)):
+            at = 2 * k + c
+            value = values[pl.ds(pl.multiple_of(at * local_rows, local_rows), local_rows), :]
+            owned[places[at]] = value
+            out[back] = value.astype(out.dtype)
+            total = total + jnp.sum(value, axis=0, keepdims=True)
+        return total
+
+    mean = lax.fori_loop(0, RING, take, mean) / count
+
+    def center(at, square):
+        span = pl.ds(pl.multiple_of(at * local_rows, local_rows), local_rows)
+        centered = values[span, :] - mean
+        rows[span, :] = centered.astype(rows.dtype)
+        return square + jnp.sum(centered * centered, axis=0, keepdims=True)
+
+    square = lax.fori_loop(0, count // local_rows, center, jnp.zeros_like(mean))
     variance[...] = square / (count - 1)
     blocks = count // GRAM_BLOCK
     half = by_y.shape[2]
@@ -427,7 +457,7 @@
     weight = gather_weight(start_weight(projector_weight, dp_index, dp_count), plane, core)
     feature_part = weight.shape[2]
     tops = (
-        plane_gather(jnp.concatenate(hidden[:2]), "mp_1", "mp_0"),
+        split_gather(hidden[0], hidden[1], "mp_1", "mp_0"),
         plane_gather(jnp.concatenate([hidden[3], hidden[2]]), "mp_0", "mp_1"),
     )
     bases = [embed(pieces, weight, x_first) for pieces, x_first in zip(tops, (True, False))]

time: 365 us -> 359 us (0.984)
  waiting for transfers between devices: 188 us -> 176 us
  starting transfers between devices: 93.8 us -> 98.8 us
    ppermute x53 -> x57, waiting for transfers between devices: 184 us -> 173 us  [shift(): return lax.ppermute(x, axis, [(i, (i + step) % RING) for i in range(RING)])]
    concatenate x0 -> x4, local copies, waits for them, and re-layouts: none -> 4.96 us  [the longest x3 3.19 us: split_gather(): jnp.concatenate(pair)]
    ppermute x53 -> x57, starting transfers between devices: 82 us -> 85.4 us  [shift(): return lax.ppermute(x, axis, [(i, (i + step) % RING) for i in range(RING)])]
    unnamed x62 -> x89, local copies, waits for them, and re-layouts: 13.1 us -> 11.2 us
  transfers between devices with their start and end apart: 61 -> 65, of which waited for: 23 -> 26; matrix products, arithmetic and copies ran while one was open for 8% -> 9% of each run, Pallas kernels for 9% -> 9%
where the time goes in v2:
time: 359 us; the launch traced here: 358 us
  waiting for transfers between devices  176 us (49%)
  starting transfers between devices  98.8 us (28%)
  Pallas kernels  41.3 us (12%)
  local copies, waits for them, and re-layouts  33.9 us (9%)
  other arithmetic  5.65 us (2%)
    ppermute x57, waiting for transfers between devices, shift(): return lax.ppermute(x, axis, [(i, (i + step) % RING) for i in range(RING)])  173 us
    ppermute x57, starting transfers between devices, shift(): return lax.ppermute(x, axis, [(i, (i + step) % RING) for i in range(RING)])  85.4 us
    pallas_call x6, Pallas kernels, matmul(): pl.pallas_call(lambda *refs: matmul_body(len(parts), base is not None, *r...  24.1 us
    unnamed x89, local copies, waits for them, and re-layouts  11.2 us
    all_to_all x1, starting transfers between devices, start_weight(): return lax.all_to_all(own, MP, split_axis=0, concat_axis=0, tiled=True)  7.24 us
  transfers between devices with their start and end apart: 65, of which 26 were waited for; matrix products, arithmetic and copies ran while one was open for 9% of the time, Pallas kernels for 9%

profile of v2, /device:TPU:0, one launch (start us, length us, event | category | flops | bytes accessed | tf_op | source)
XLA Modules:
  0.0 357.6 jit_solution(6661939302096814927)
XLA Ops:
  4.9 4.2 %collective-permute-start.27 = (bf16[2,192,512]{2,1,0:T(8,128)(2,1)S(1)}, bf16[2,192,512]{2,1,0:T(8,128)(2,1)S(1)}, u32[]{:S(2)}, u32[]{:S(2)}) collective-permute-start(bf16[2,192,512]{2,1,0:T(8,128)(2,1)S(1)} %get-tuple-element.23), channel_id=1, source_target_pairs={{0,96},{32,0},{64,32},{96,64},{1,97},{33,1},{65,33},{97,65},{2,98}... | collective-permute-start | bytes 1179656 | tf_op jit(solution)/shard_map/ppermute | solution.py:20
  13.6 12.6 %collective-permute-done.27 = bf16[2,192,512]{2,1,0:T(8,128)(2,1)S(1)} collective-permute-done((bf16[2,192,512]{2,1,0:T(8,128)(2,1)S(1)}, bf16[2,192,512]{2,1,0:T(8,128)(2,1)S(1)}, u32[]{:S(2)}, u32[]{:S(2)}) %collective-permute-start.27) | collective-permute-done | bytes 393248 | tf_op jit(solution)/shard_map/ppermute | solution.py:20
  34.9 7.2 %all-to-all-start = ((bf16[16,64,512]{2,1,0:T(8,128)(2,1)}), bf16[16,64,512]{2,1,0:T(8,128)(2,1)S(1)}, u32[]{:S(2)}, u32[]{:S(2)}) async-start(bf16[16,64,512]{2,1,0:T(8,128)(2,1)} %bitcast.81), calls=%async_computation | async-start | bytes 2097152 | tf_op jit(solution)/shard_map/all_to_all | solution.py:59
  50.5 14.4 %collective-permute-done.17 = bf16[384,512]{1,0:T(8,128)(2,1)S(1)} collective-permute-done((bf16[384,512]{1,0:T(8,128)(2,1)}, bf16[384,512]{1,0:T(8,128)(2,1)S(1)}, u32[]{:S(2)}, u32[]{:S(2)}) %collective-permute-start.17) | collective-permute-done | bytes 393248 | tf_op jit(solution)/shard_map/ppermute | solution.py:20
  69.7 12.1 %collective-permute-done.10 = bf16[384,512]{1,0:T(8,128)(2,1)} collective-permute-done((bf16[384,512]{1,0:T(8,128)(2,1)}, bf16[384,512]{1,0:T(8,128)(2,1)}, u32[]{:S(2)}, u32[]{:S(2)}) %collective-permute-start.10) | collective-permute-done | bytes 393248 | tf_op jit(solution)/shard_map/ppermute | solution.py:20
  81.8 3.7 %collective-permute-start.3 = (bf16[16,64,512]{2,1,0:T(8,128)(2,1)S(1)}, bf16[16,64,512]{2,1,0:T(8,128)(2,1)}, u32[]{:S(2)}, u32[]{:S(2)}) collective-permute-start(bf16[16,64,512]{2,1,0:T(8,128)(2,1)S(1)} %all-to-all-done.refs_0_), channel_id=1, source_target_pairs={{0,64},{32,96},{64,0},{96,32},{1,65},{33,97},{65,1},{97,33},{2,66}... | collective-permute-start | bytes 3145736 | tf_op jit(solution)/shard_map/ppermute | solution.py:20
  90.2 7.2 %collective-permute-done.21 = bf16[384,512]{1,0:T(8,128)(2,1)S(1)} collective-permute-done((bf16[384,512]{1,0:T(8,128)(2,1)}, bf16[384,512]{1,0:T(8,128)(2,1)S(1)}, u32[]{:S(2)}, u32[]{:S(2)}) %collective-permute-start.21) | collective-permute-done | bytes 393248 | tf_op jit(solution)/shard_map/ppermute | solution.py:20
  98.6 11.0 %collective-permute-done.1.refs_2_ = bf16[16,64,512]{2,1,0:T(8,128)(2,1)} collective-permute-done((bf16[16,64,512]{2,1,0:T(8,128)(2,1)S(1)}, bf16[16,64,512]{2,1,0:T(8,128)(2,1)}, u32[]{:S(2)}, u32[]{:S(2)}) %collective-permute-start.1) | collective-permute-done | bytes 1048608 | tf_op jit(solution)/shard_map/ppermute | solution.py:20
  110.2 19.5 %collective-permute-done.3.refs_4_ = bf16[16,64,512]{2,1,0:T(8,128)(2,1)} collective-permute-done((bf16[16,64,512]{2,1,0:T(8,128)(2,1)S(1)}, bf16[16,64,512]{2,1,0:T(8,128)(2,1)}, u32[]{:S(2)}, u32[]{:S(2)}) %collective-permute-start.3) | collective-permute-done | bytes 1048608 | tf_op jit(solution)/shard_map/ppermute | solution.py:20
  135.5 5.9 %collective-permute-done.37 = bf16[384,512]{1,0:T(8,128)(2,1)S(1)} collective-permute-done((bf16[384,512]{1,0:T(8,128)(2,1)S(1)}, bf16[384,512]{1,0:T(8,128)(2,1)S(1)}, u32[]{:S(2)}, u32[]{:S(2)}) %collective-permute-start.37) | collective-permute-done | bytes 393248 | tf_op jit(solution)/shard_map/ppermute | solution.py:20
  141.4 14.0 %collective-permute-done.38 = bf16[384,512]{1,0:T(8,128)(2,1)S(1)} collective-permute-done((bf16[384,512]{1,0:T(8,128)(2,1)S(1)}, bf16[384,512]{1,0:T(8,128)(2,1)S(1)}, u32[]{:S(2)}, u32[]{:S(2)}) %collective-permute-start.38) | collective-permute-done | bytes 393248 | tf_op jit(solution)/shard_map/ppermute | solution.py:20
  156.4 11.0 %collective-permute-start.32 = (bf16[768,512]{1,0:T(8,128)(2,1)S(1)}, bf16[768,512]{1,0:T(8,128)(2,1)S(1)}, u32[]{:S(2)}, u32[]{:S(2)}) collective-permute-start(bf16[768,512]{1,0:T(8,128)(2,1)S(1)} %copy-done.1), channel_id=1, source_target_pairs={{0,3},{1,0},{2,1},{3,2},{4,7},{5,4},{6,5},{7,6},{8,11},{9,8},{10,9... | collective-permute-start | bytes 2359304 | tf_op jit(solution)/shard_map/ppermute | solution.py:20
  169.3 6.7 %collective-permute-done.11.refs_1_ = bf16[768,512]{1,0:T(8,128)(2,1)S(1)} collective-permute-done((bf16[768,512]{1,0:T(8,128)(2,1)S(1)}, bf16[768,512]{1,0:T(8,128)(2,1)S(1)}, u32[]{:S(2)}, u32[]{:S(2)}) %collective-permute-start.11) | collective-permute-done | bytes 786464 | tf_op jit(solution)/shard_map/ppermute | solution.py:20
  177.4 11.3 %collective-permute-done.35.refs_2_ = bf16[768,512]{1,0:T(8,128)(2,1)S(1)} collective-permute-done((bf16[768,512]{1,0:T(8,128)(2,1)S(1)}, bf16[768,512]{1,0:T(8,128)(2,1)S(1)}, u32[]{:S(2)}, u32[]{:S(2)}) %collective-permute-start.35) | collective-permute-done | bytes 786464 | tf_op jit(solution)/shard_map/ppermute | solution.py:20
  188.7 13.0 %collective-permute-done.36.refs_3_ = bf16[768,512]{1,0:T(8,128)(2,1)S(1)} collective-permute-done((bf16[768,512]{1,0:T(8,128)(2,1)S(1)}, bf16[768,512]{1,0:T(8,128)(2,1)S(1)}, u32[]{:S(2)}, u32[]{:S(2)}) %collective-permute-start.36) | collective-permute-done | bytes 786464 | tf_op jit(solution)/shard_map/ppermute | solution.py:20
  209.1 10.9 %collective-permute-done.30.refs_1_ = bf16[768,512]{1,0:T(8,128)(2,1)} collective-permute-done((bf16[768,512]{1,0:T(8,128)(2,1)}, bf16[768,512]{1,0:T(8,128)(2,1)}, u32[]{:S(2)}, u32[]{:S(2)}) %collective-permute-start.30) | collective-permute-done | bytes 786464 | tf_op jit(solution)/shard_map/ppermute | solution.py:20
  220.0 6.1 %collective-permute-start.26 = (bf16[768,512]{1,0:T(8,128)(2,1)}, bf16[768,512]{1,0:T(8,128)(2,1)}, u32[]{:S(2)}, u32[]{:S(2)}) collective-permute-start(bf16[768,512]{1,0:T(8,128)(2,1)} %constant_dynamic-update-slice_fusion.6.refs_4_), channel_id=1, source_target_pairs={{0,12},{4,0},{8,4},{12,8},{1,13},{5,1},{9,5},{13,9},{2,14},{6,2},{... | collective-permute-start | bytes 2359304 | tf_op jit(solution)/shard_map/ppermute | solution.py:20
  226.1 3.2 collective-permute-start.42
  234.0 3.8 %assemble.1.refs_5_.refs_9_.refs_3_ = bf16[16,512,512]{2,1,0:T(8,128)(2,1)S(1)} custom-call(s32[8]{0:T(128)S(1)} %stack.186.places, bf16[16,64,512]{2,1,0:T(8,128)(2,1)S(1)} %all-to-all-done.refs_0_, bf16[16,64,512]{2,1,0:T(8,128)(2,1)S(1)} %copy-done.10, bf16[16,64,512]{2,1,0:T(8,128)(2,1)} %collective-permute-done.1.refs_2_, ...), custom_call_target="tpu_custom_call" | custom-call | tf_op jit(solution)/shard_map/assemble/pallas_call | solution.py:43
  237.9 3.6 %embed.6.refs_10_ = f32[768,512]{1,0:T(8,128)S(1)} custom-call(s32[4]{0:T(128)S(1)} %pad_add_fusion.5.refs_0_, bf16[768,512]{1,0:T(8,128)(2,1)S(1)} %pad_maximum_fusion.3.refs_1_, bf16[768,512]{1,0:T(8,128)(2,1)S(1)} %copy-done.4, bf16[768,512]{1,0:T(8,128)(2,1)S(1)} %copy-done.6, bf16[768,512]{1,0:T(8,128)(2,1)} %constant_dynamic-update-slice_fusion.6.refs_4_, ...), custom_call_target="tpu_custom_call" | custom-call | flops 1610612736 | bytes 6815744 | tf_op jit(solution)/shard_map/embed/pallas_call | solution.py:165
  249.5 3.3 collective-permute-done.15.refs_2_
  252.9 3.5 embed.9.refs_10_
  256.4 5.6 %embed.7.refs_4_ = f32[768,512]{1,0:T(8,128)S(1)} custom-call(s32[8]{0:T(128)S(1)} %stack.199.refs_0_, bf16[768,512]{1,0:T(8,128)(2,1)S(1)} %constant_dynamic-update-slice_fusion.refs_1_, bf16[768,512]{1,0:T(8,128)(2,1)S(1)} %copy-done.12, bf16[768,512]{1,0:T(8,128)(2,1)S(1)} %copy-done.20, bf16[768,512]{1,0:T(8,128)(2,1)} %collective-permute-done.22.refs_4_, ...), custom_call_target="tpu_custom_call" | custom-call | flops 3221225472 | bytes 12058624 | tf_op jit(solution)/shard_map/embed/pallas_call | solution.py:165
  264.8 6.0 %embed.10.refs_4_ = f32[768,512]{1,0:T(8,128)S(1)} custom-call(s32[8]{0:T(128)S(1)} %stack.206.refs_0_, bf16[768,512]{1,0:T(8,128)(2,1)} %collective-permute-done.29.refs_1_, bf16[768,512]{1,0:T(8,128)(2,1)S(1)} %copy-done.16, bf16[768,512]{1,0:T(8,128)(2,1)S(1)} %copy-done.22, bf16[768,512]{1,0:T(8,128)(2,1)} %collective-permute-done.39.refs_4_, ...), custom_call_target="tpu_custom_call" | custom-call | flops 3221225472 | bytes 12058624 | tf_op jit(solution)/shard_map/embed/pallas_call | solution.py:165
  273.6 6.1 %finish.1 = (f32[8,192,512]{2,1,0:T(8,128)S(1)}, bf16[4,192,512]{2,1,0:T(8,128)(2,1)S(1)}, bf16[4,192,512]{2,1,0:T(8,128)(2,1)}, bf16[4,4,320,128]{3,2,1,0:T(8,1...) custom-call(s32[2]{0:T(128)S(1)} %get-tuple-element.68.refs_0_, ...), custom_call_target="tpu_custom_call" | custom-call | flops 2415919104 | bytes 6291456 | tf_op jit(solution)/shard_map/finish/pallas_call | solution.py:277
  292.1 11.5 %collective-permute-done.57 = bf16[4,320,128]{2,1,0:T(8,128)(2,1)} collective-permute-done((bf16[4,320,128]{2,1,0:T(8,128)(2,1)}, bf16[4,320,128]{2,1,0:T(8,128)(2,1)}, u32[]{:S(2)}, u32[]{:S(2)}) %collective-permute-start.57) | collective-permute-done | bytes 327712 | tf_op jit(solution)/shard_map/ppermute | solution.py:20
  303.6 3.7 %collective-permute-start.52 = (bf16[4,320,128]{2,1,0:T(8,128)(2,1)}, bf16[4,320,128]{2,1,0:T(8,128)(2,1)S(1)}, u32[]{:S(2)}, u32[]{:S(2)}) collective-permute-start(bf16[4,320,128]{2,1,0:T(8,128)(2,1)} %get-tuple-element.51), channel_id=1, source_target_pairs={{0,12},{4,0},{8,4},{12,8},{1,13},{5,1},{9,5},{13,9},{2,14},{6,2},{... | collective-permute-start | bytes 983048 | tf_op jit(solution)/shard_map/ppermute | solution.py:20
  313.4 8.1 %collective-permute-done.52 = bf16[4,320,128]{2,1,0:T(8,128)(2,1)S(1)} collective-permute-done((bf16[4,320,128]{2,1,0:T(8,128)(2,1)}, bf16[4,320,128]{2,1,0:T(8,128)(2,1)S(1)}, u32[]{:S(2)}, u32[]{:S(2)}) %collective-permute-start.52) | collective-permute-done | bytes 327712 | tf_op jit(solution)/shard_map/ppermute | solution.py:20
  321.4 3.6 %collective-permute-start.61 = (bf16[320,128]{1,0:T(8,128)(2,1)S(1)}, bf16[320,128]{1,0:T(8,128)(2,1)S(1)}, u32[]{:S(2)}, u32[]{:S(2)}) collective-permute-start(bf16[320,128]{1,0:T(8,128)(2,1)S(1)} %get-tuple-element.53), channel_id=1, source_target_pairs={{0,12},{4,0},{8,4},{12,8},{1,13},{5,1},{9,5},{13,9},{2,14},{6,2},{... | collective-permute-start | bytes 245768 | tf_op jit(solution)/shard_map/ppermute | solution.py:20
  330.1 3.2 collective-permute-start.55
  341.4 5.4 %all-to-all-start.1 = ((f32[128,1,128]{2,1,0:T(1,128)}), f32[128,1,128]{2,1,0:T(1,128)S(1)}, u32[]{:S(2)}, u32[]{:S(2)}) async-start(f32[128,1,128]{2,1,0:T(1,128)} %bitcast.55), calls=%async_computation.1 | async-start | bytes 131072 | tf_op jit(solution)/shard_map/all_to_all | solution.py:358
  349.3 5.7 %broadcast_in_dim.3 = f32[512,1,1536]{2,1,0:T(1,128)} reshape(f32[512,1536]{1,0:T(8,128)} %bitcast.89) | data formatting | bytes 6291456 | tf_op jit(solution)/shard_map/broadcast_in_dim | solution.py:487
  (234 shorter events, 108.8 us)
Async XLA Ops:
  4.9 21.3 %collective-permute-start.27 = (bf16[2,192,512]{2,1,0:T(8,128)(2,1)S(1)}, bf16[2,192,512]{2,1,0:T(8,128)(2,1)S(1)}, u32[]{:S(2)}, u32[]{:S(2)}) collective-permute-start(bf16[2,192,512]{2,1,0:T(8,128)(2,1)S(1)} %get-tuple-element.23), channel_id=1, source_target_pairs={{0,96},{32,0},{64,32},{96,64},{1,97},{33,1},{65,33},{97,65},{2,98}... | collective-permute-start | bytes 1179656 | tf_op jit(solution)/shard_map/ppermute | solution.py:20
  10.4 22.1 %collective-permute-start.16 = (bf16[384,512]{1,0:T(8,128)(2,1)S(1)}, bf16[384,512]{1,0:T(8,128)(2,1)}, u32[]{:S(2)}, u32[]{:S(2)}) collective-permute-start(bf16[384,512]{1,0:T(8,128)(2,1)S(1)} %bitcast.83), channel_id=1, source_target_pairs={{0,1},{1,2},{2,3},{3,0},{4,5},{5,6},{6,7},{7,4},{8,9},{9,10},{10,1... | collective-permute-start | bytes 1179656 | tf_op jit(solution)/shard_map/ppermute | solution.py:20
  11.9 30.3 %collective-permute-start.12 = (bf16[384,512]{1,0:T(8,128)(2,1)S(1)}, bf16[384,512]{1,0:T(8,128)(2,1)S(1)}, u32[]{:S(2)}, u32[]{:S(2)}) collective-permute-start(bf16[384,512]{1,0:T(8,128)(2,1)S(1)} %bitcast.84), channel_id=1, source_target_pairs={{0,3},{1,0},{2,1},{3,2},{4,7},{5,4},{6,5},{7,6},{8,11},{9,8},{10,9... | collective-permute-start | bytes 1179656 | tf_op jit(solution)/shard_map/ppermute | solution.py:20
  34.9 34.9 %all-to-all-start = ((bf16[16,64,512]{2,1,0:T(8,128)(2,1)}), bf16[16,64,512]{2,1,0:T(8,128)(2,1)S(1)}, u32[]{:S(2)}, u32[]{:S(2)}) async-start(bf16[16,64,512]{2,1,0:T(8,128)(2,1)} %bitcast.81), calls=%async_computation | async-start | bytes 2097152 | tf_op jit(solution)/shard_map/all_to_all | solution.py:59
  42.1 22.8 %collective-permute-start.17 = (bf16[384,512]{1,0:T(8,128)(2,1)}, bf16[384,512]{1,0:T(8,128)(2,1)S(1)}, u32[]{:S(2)}, u32[]{:S(2)}) collective-permute-start(bf16[384,512]{1,0:T(8,128)(2,1)} %bitcast.22), channel_id=1, source_target_pairs={{0,1},{1,2},{2,3},{3,0},{4,5},{5,6},{6,7},{7,4},{8,9},{9,10},{10,1... | collective-permute-start | bytes 1179656 | tf_op jit(solution)/shard_map/ppermute | solution.py:20
  44.2 37.6 %collective-permute-start.34 = (bf16[768,512]{1,0:T(8,128)(2,1)S(1)}, bf16[768,512]{1,0:T(8,128)(2,1)S(1)}, u32[]{:S(2)}, u32[]{:S(2)}) collective-permute-start(bf16[768,512]{1,0:T(8,128)(2,1)S(1)} %pad_maximum_fusion.4.refs_1_), channel_id=1, source_target_pairs={{0,4},{4,8},{8,12},{12,0},{1,5},{5,9},{9,13},{13,1},{2,6},{6,10},{... | collective-permute-start | bytes 2359304 | tf_op jit(solution)/shard_map/ppermute | solution.py:20
  47.5 38.0 %collective-permute-start.31 = (bf16[768,512]{1,0:T(8,128)(2,1)S(1)}, bf16[768,512]{1,0:T(8,128)(2,1)S(1)}, u32[]{:S(2)}, u32[]{:S(2)}) collective-permute-start(bf16[768,512]{1,0:T(8,128)(2,1)S(1)} %pad_maximum_fusion.4.refs_1_), channel_id=1, source_target_pairs={{0,12},{4,0},{8,4},{12,8},{1,13},{5,1},{9,5},{13,9},{2,14},{6,2},{... | collective-permute-start | bytes 2359304 | tf_op jit(solution)/shard_map/ppermute | solution.py:20
  49.1 36.5 %collective-permute-start.29 = (bf16[768,512]{1,0:T(8,128)(2,1)S(1)}, bf16[768,512]{1,0:T(8,128)(2,1)}, u32[]{:S(2)}, u32[]{:S(2)}) collective-permute-start(bf16[768,512]{1,0:T(8,128)(2,1)S(1)} %pad_maximum_fusion.4.refs_1_), channel_id=1, source_target_pairs={{0,1},{1,2},{2,3},{3,0},{4,5},{5,6},{6,7},{7,4},{8,9},{9,10},{10,1... | collective-permute-start | bytes 2359304 | tf_op jit(solution)/shard_map/ppermute | solution.py:20
  81.8 27.7 %collective-permute-start.1 = (bf16[16,64,512]{2,1,0:T(8,128)(2,1)S(1)}, bf16[16,64,512]{2,1,0:T(8,128)(2,1)}, u32[]{:S(2)}, u32[]{:S(2)}) collective-permute-start(bf16[16,64,512]{2,1,0:T(8,128)(2,1)S(1)} %all-to-all-done.refs_0_), channel_id=1, source_target_pairs={{0,32},{32,64},{64,96},{96,0},{1,33},{33,65},{65,97},{97,1},{2,34}... | collective-permute-start | bytes 3145736 | tf_op jit(solution)/shard_map/ppermute | solution.py:20
  81.8 47.9 %collective-permute-start.3 = (bf16[16,64,512]{2,1,0:T(8,128)(2,1)S(1)}, bf16[16,64,512]{2,1,0:T(8,128)(2,1)}, u32[]{:S(2)}, u32[]{:S(2)}) collective-permute-start(bf16[16,64,512]{2,1,0:T(8,128)(2,1)S(1)} %all-to-all-done.refs_0_), channel_id=1, source_target_pairs={{0,64},{32,96},{64,0},{96,32},{1,65},{33,97},{65,1},{97,33},{2,66}... | collective-permute-start | bytes 3145736 | tf_op jit(solution)/shard_map/ppermute | solution.py:20
  85.5 45.6 %collective-permute-start.5 = (bf16[16,64,512]{2,1,0:T(8,128)(2,1)S(1)}, bf16[16,64,512]{2,1,0:T(8,128)(2,1)}, u32[]{:S(2)}, u32[]{:S(2)}) collective-permute-start(bf16[16,64,512]{2,1,0:T(8,128)(2,1)S(1)} %all-to-all-done.refs_0_), channel_id=1, source_target_pairs={{0,96},{32,0},{64,32},{96,64},{1,97},{33,1},{65,33},{97,65},{2,98}... | collective-permute-start | bytes 3145736 | tf_op jit(solution)/shard_map/ppermute | solution.py:20
  85.6 46.4 %collective-permute-start = (bf16[16,64,512]{2,1,0:T(8,128)(2,1)S(1)}, bf16[16,64,512]{2,1,0:T(8,128)(2,1)S(1)}, u32[]{:S(2)}, u32[]{:S(2)}) collective-permute-start(bf16[16,64,512]{2,1,0:T(8,128)(2,1)S(1)} %all-to-all-done.refs_0_), channel_id=1, source_target_pairs={{0,16},{16,0},{1,17},{17,1},{2,18},{18,2},{3,19},{19,3},{4,20},{20... | collective-permute-start | bytes 3145736 | tf_op jit(solution)/shard_map/ppermute | solution.py:24
  97.4 59.0 %collective-permute-start.18 = (bf16[768,512]{1,0:T(8,128)(2,1)S(1)}, bf16[768,512]{1,0:T(8,128)(2,1)S(1)}, u32[]{:S(2)}, u32[]{:S(2)}) collective-permute-start(bf16[768,512]{1,0:T(8,128)(2,1)S(1)} %constant_dynamic-update-slice_fusion.4.refs_2_), channel_id=1, source_target_pairs={{0,4},{4,8},{8,12},{12,0},{1,5},{5,9},{9,13},{13,1},{2,6},{6,10},{... | collective-permute-start | bytes 2359304 | tf_op jit(solution)/shard_map/ppermute | solution.py:20
  109.6 57.8 %collective-permute-start.25 = (bf16[768,512]{1,0:T(8,128)(2,1)S(1)}, bf16[768,512]{1,0:T(8,128)(2,1)S(1)}, u32[]{:S(2)}, u32[]{:S(2)}) collective-permute-start(bf16[768,512]{1,0:T(8,128)(2,1)S(1)} %constant_dynamic-update-slice_fusion.4.refs_2_), channel_id=1, source_target_pairs={{0,12},{4,0},{8,4},{12,8},{1,13},{5,1},{9,5},{13,9},{2,14},{6,2},{... | collective-permute-start | bytes 2359304 | tf_op jit(solution)/shard_map/ppermute | solution.py:20
  129.7 38.5 %collective-permute-start.14 = (bf16[768,512]{1,0:T(8,128)(2,1)S(1)}, bf16[768,512]{1,0:T(8,128)(2,1)}, u32[]{:S(2)}, u32[]{:S(2)}) collective-permute-start(bf16[768,512]{1,0:T(8,128)(2,1)S(1)} %constant_dynamic-update-slice_fusion.2.refs_3_), channel_id=1, source_target_pairs={{0,12},{4,0},{8,4},{12,8},{1,13},{5,1},{9,5},{13,9},{2,14},{6,2},{... | collective-permute-start | bytes 2359304 | tf_op jit(solution)/shard_map/ppermute | solution.py:20
  132.0 23.4 %collective-permute-start.38 = (bf16[384,512]{1,0:T(8,128)(2,1)S(1)}, bf16[384,512]{1,0:T(8,128)(2,1)S(1)}, u32[]{:S(2)}, u32[]{:S(2)}) collective-permute-start(bf16[384,512]{1,0:T(8,128)(2,1)S(1)} %slice.9), channel_id=1, source_target_pairs={{0,12},{4,0},{8,4},{12,8},{1,13},{5,1},{9,5},{13,9},{2,14},{6,2},{... | collective-permute-start | bytes 1179656 | tf_op jit(solution)/shard_map/ppermute | solution.py:20
  141.4 27.0 %collective-permute-start.19 = (bf16[768,512]{1,0:T(8,128)(2,1)S(1)}, bf16[768,512]{1,0:T(8,128)(2,1)S(1)}, u32[]{:S(2)}, u32[]{:S(2)}) collective-permute-start(bf16[768,512]{1,0:T(8,128)(2,1)S(1)} %constant_dynamic-update-slice_fusion.2.refs_3_), channel_id=1, source_target_pairs={{0,4},{4,8},{8,12},{12,0},{1,5},{5,9},{9,13},{13,1},{2,6},{6,10},{... | collective-permute-start | bytes 2359304 | tf_op jit(solution)/shard_map/ppermute | solution.py:20
  168.2 33.4 %collective-permute-start.36 = (bf16[768,512]{1,0:T(8,128)(2,1)S(1)}, bf16[768,512]{1,0:T(8,128)(2,1)S(1)}, u32[]{:S(2)}, u32[]{:S(2)}) collective-permute-start(bf16[768,512]{1,0:T(8,128)(2,1)S(1)} %copy-done.1), channel_id=1, source_target_pairs={{0,1},{1,2},{2,3},{3,0},{4,5},{5,6},{6,7},{7,4},{8,9},{9,10},{10,1... | collective-permute-start | bytes 2359304 | tf_op jit(solution)/shard_map/ppermute | solution.py:20
  169.3 56.8 %collective-permute-start.2 = (bf16[16,64,512]{2,1,0:T(8,128)(2,1)}, bf16[16,64,512]{2,1,0:T(8,128)(2,1)}, u32[]{:S(2)}, u32[]{:S(2)}) collective-permute-start(bf16[16,64,512]{2,1,0:T(8,128)(2,1)} %collective-permute-done.1.refs_2_), channel_id=1, source_target_pairs={{0,16},{16,0},{1,17},{17,1},{2,18},{18,2},{3,19},{19,3},{4,20},{20... | collective-permute-start | bytes 3145736 | tf_op jit(solution)/shard_map/ppermute | solution.py:24
  176.9 49.2 %collective-permute-start.4 = (bf16[16,64,512]{2,1,0:T(8,128)(2,1)}, bf16[16,64,512]{2,1,0:T(8,128)(2,1)}, u32[]{:S(2)}, u32[]{:S(2)}) collective-permute-start(bf16[16,64,512]{2,1,0:T(8,128)(2,1)} %collective-permute-done.3.refs_4_), channel_id=1, source_target_pairs={{0,16},{16,0},{1,17},{17,1},{2,18},{18,2},{3,19},{19,3},{4,20},{20... | collective-permute-start | bytes 3145736 | tf_op jit(solution)/shard_map/ppermute | solution.py:24
  176.9 52.4 %collective-permute-start.6 = (bf16[16,64,512]{2,1,0:T(8,128)(2,1)}, bf16[16,64,512]{2,1,0:T(8,128)(2,1)}, u32[]{:S(2)}, u32[]{:S(2)}) collective-permute-start(bf16[16,64,512]{2,1,0:T(8,128)(2,1)} %collective-permute-done.5.refs_6_), channel_id=1, source_target_pairs={{0,16},{16,0},{1,17},{17,1},{2,18},{18,2},{3,19},{19,3},{4,20},{20... | collective-permute-start | bytes 3145736 | tf_op jit(solution)/shard_map/ppermute | solution.py:24
  207.9 33.6 %collective-permute-start.22 = (bf16[768,512]{1,0:T(8,128)(2,1)}, bf16[768,512]{1,0:T(8,128)(2,1)}, u32[]{:S(2)}, u32[]{:S(2)}) collective-permute-start(bf16[768,512]{1,0:T(8,128)(2,1)} %constant_dynamic-update-slice_fusion.6.refs_4_), channel_id=1, source_target_pairs={{0,4},{4,8},{8,12},{12,0},{1,5},{5,9},{9,13},{13,1},{2,6},{6,10},{... | collective-permute-start | bytes 2359304 | tf_op jit(solution)/shard_map/ppermute | solution.py:20
  220.0 23.8 %collective-permute-start.26 = (bf16[768,512]{1,0:T(8,128)(2,1)}, bf16[768,512]{1,0:T(8,128)(2,1)}, u32[]{:S(2)}, u32[]{:S(2)}) collective-permute-start(bf16[768,512]{1,0:T(8,128)(2,1)} %constant_dynamic-update-slice_fusion.6.refs_4_), channel_id=1, source_target_pairs={{0,12},{4,0},{8,4},{12,8},{1,13},{5,1},{9,5},{13,9},{2,14},{6,2},{... | collective-permute-start | bytes 2359304 | tf_op jit(solution)/shard_map/ppermute | solution.py:20
  226.1 21.5 %collective-permute-start.42 = (bf16[768,512]{1,0:T(8,128)(2,1)}, bf16[768,512]{1,0:T(8,128)(2,1)}, u32[]{:S(2)}, u32[]{:S(2)}) collective-permute-start(bf16[768,512]{1,0:T(8,128)(2,1)} %constant_dynamic-update-slice_fusion.8.refs_4_), channel_id=1, source_target_pairs={{0,3},{1,0},{2,1},{3,2},{4,7},{5,4},{6,5},{7,6},{8,11},{9,8},{10,9... | collective-permute-start | bytes 2359304 | tf_op jit(solution)/shard_map/ppermute | solution.py:20
  229.4 23.4 %collective-permute-start.15 = (bf16[768,512]{1,0:T(8,128)(2,1)}, bf16[768,512]{1,0:T(8,128)(2,1)}, u32[]{:S(2)}, u32[]{:S(2)}) collective-permute-start(bf16[768,512]{1,0:T(8,128)(2,1)} %collective-permute-done.14.refs_7_), channel_id=1, source_target_pairs={{0,12},{4,0},{8,4},{12,8},{1,13},{5,1},{9,5},{13,9},{2,14},{6,2},{... | collective-permute-start | bytes 2359304 | tf_op jit(solution)/shard_map/ppermute | solution.py:20
  241.6 32.0 %collective-permute-start.43 = (bf16[768,512]{1,0:T(8,128)(2,1)S(1)}, bf16[768,512]{1,0:T(8,128)(2,1)S(1)}, u32[]{:S(2)}, u32[]{:S(2)}) collective-permute-start(bf16[768,512]{1,0:T(8,128)(2,1)S(1)} %copy-done.12), channel_id=1, source_target_pairs={{0,4},{4,8},{8,12},{12,0},{1,5},{5,9},{9,13},{13,1},{2,6},{6,10},{... | collective-permute-start | bytes 2359304 | tf_op jit(solution)/shard_map/ppermute | solution.py:20
  243.8 27.1 %collective-permute-start.33 = (bf16[768,512]{1,0:T(8,128)(2,1)S(1)}, bf16[768,512]{1,0:T(8,128)(2,1)S(1)}, u32[]{:S(2)}, u32[]{:S(2)}) collective-permute-start(bf16[768,512]{1,0:T(8,128)(2,1)S(1)} %copy-done.18), channel_id=1, source_target_pairs={{0,3},{1,0},{2,1},{3,2},{4,7},{5,4},{6,5},{7,6},{8,11},{9,8},{10,9... | collective-permute-start | bytes 2359304 | tf_op jit(solution)/shard_map/ppermute | solution.py:20
  245.1 28.4 %collective-permute-start.45 = (bf16[768,512]{1,0:T(8,128)(2,1)S(1)}, bf16[768,512]{1,0:T(8,128)(2,1)S(1)}, u32[]{:S(2)}, u32[]{:S(2)}) collective-permute-start(bf16[768,512]{1,0:T(8,128)(2,1)S(1)} %copy-done.16), channel_id=1, source_target_pairs={{0,1},{1,2},{2,3},{3,0},{4,5},{5,6},{6,7},{7,4},{8,9},{9,10},{10,1... | collective-permute-start | bytes 2359304 | tf_op jit(solution)/shard_map/ppermute | solution.py:20
  247.6 25.9 %collective-permute-start.44 = (bf16[768,512]{1,0:T(8,128)(2,1)}, bf16[768,512]{1,0:T(8,128)(2,1)S(1)}, u32[]{:S(2)}, u32[]{:S(2)}) collective-permute-start(bf16[768,512]{1,0:T(8,128)(2,1)} %collective-permute-done.26.refs_8_), channel_id=1, source_target_pairs={{0,12},{4,0},{8,4},{12,8},{1,13},{5,1},{9,5},{13,9},{2,14},{6,2},{... | collective-permute-start | bytes 2359304 | tf_op jit(solution)/shard_map/ppermute | solution.py:20
  252.8 20.8 %collective-permute-start.46 = (bf16[768,512]{1,0:T(8,128)(2,1)}, bf16[768,512]{1,0:T(8,128)(2,1)S(1)}, u32[]{:S(2)}, u32[]{:S(2)}) collective-permute-start(bf16[768,512]{1,0:T(8,128)(2,1)} %collective-permute-done.42.refs_8_), channel_id=1, source_target_pairs={{0,3},{1,0},{2,1},{3,2},{4,7},{5,4},{6,5},{7,6},{8,11},{9,8},{10,9... | collective-permute-start | bytes 2359304 | tf_op jit(solution)/shard_map/ppermute | solution.py:20
  282.7 26.1 %collective-permute-start.47 = (bf16[4,192,512]{2,1,0:T(8,128)(2,1)}, bf16[4,192,512]{2,1,0:T(8,128)(2,1)}, u32[]{:S(2)}, u32[]{:S(2)}) collective-permute-start(bf16[4,192,512]{2,1,0:T(8,128)(2,1)} %get-tuple-element.30), channel_id=1, source_target_pairs={{0,16},{16,0},{1,17},{17,1},{2,18},{18,2},{3,19},{19,3},{4,20},{20... | collective-permute-start | bytes 2359304 | tf_op jit(solution)/shard_map/ppermute | solution.py:24
  310.2 23.2 %collective-permute-start.50 = (bf16[2,192,512]{2,1,0:T(8,128)(2,1)S(1)}, bf16[2,192,512]{2,1,0:T(8,128)(2,1)S(1)}, u32[]{:S(2)}, u32[]{:S(2)}) collective-permute-start(bf16[2,192,512]{2,1,0:T(8,128)(2,1)S(1)} %get-tuple-element.34), channel_id=1, source_target_pairs={{0,96},{32,0},{64,32},{96,64},{1,97},{33,1},{65,33},{97,65},{2,98}... | collective-permute-start | bytes 1179656 | tf_op jit(solution)/shard_map/ppermute | solution.py:20
  (75 other events, 1311.8 us)
